TPU v7x, 128 devices: a whole 4x4x4 slice. The times are simulated.
128 devices in a mesh: mem: 8 (over z, x_hi), lat: 16 (over x_lo, y, core).
Axes of the slice: x: 4 (x_hi: 2, x_lo: 2; x = x_hi * 2 + x_lo), y: 4, z: 4, core: 2. Of those that a mesh axis runs over, the one named last changes fastest.
Arguments:
- features: bfloat16 [32, 32, 1440, 128], P('mem', 'lat'), may hold values from -6 to 6
- conv_inner: bfloat16 [3, 3, 128, 128], replicated, may hold values from -0.1875 to 0.1875
- conv_head: bfloat16 [3, 3, 128, 69], replicated, may hold values from -0.1875 to 0.1875
- truth: float32 [69, 32, 1440], P(None, 'lat'), may hold values from -5 to 5
- kernel_width: float32 [69], replicated, may hold values from 0.3 to 1.5
- var_weight: float32 [69], replicated, may hold values from 0.5 to 2
Outputs:
- grad_features: bfloat16 [32, 32, 1440, 128], P('mem', 'lat')
- grad_inner: float32 [3, 3, 128, 128], replicated
- grad_head: float32 [3, 3, 128, 69], replicated
All inputs are finite; a program needn't handle non-finite values.
Results may differ from a plain program's by a relative error of at most 0.0098.
Values may be sent and summed in bfloat16 or wider, within the bound.
A program may use at most 256 MiB of HBM per device.

v0:
```python
import jax
import jax.numpy as jnp
from jax import lax
from jax.sharding import PartitionSpec as P


def padded_2(cells, sides, width):
    for axis, dim in sides:
        count = lax.axis_size(axis)
        ends = count - 1
        head = lax.slice_in_dim(cells, 0, width, axis=dim)
        tail = lax.slice_in_dim(cells, cells.shape[dim] - width, cells.shape[dim], axis=dim)
        cells = jnp.concatenate(
            [
                lax.ppermute(tail, axis, [(i, (i + 1) % count) for i in range(ends)]),
                cells,
                lax.ppermute(head, axis, [((i + 1) % count, i) for i in range(ends)]),
            ],
            axis=dim,
        )
    return cells


def wrap_lon(values, axis):
    count = values.shape[axis]
    return jnp.concatenate(
        [
            lax.slice_in_dim(values, count - 1, count, axis=axis),
            values,
            lax.slice_in_dim(values, 0, 1, axis=axis),
        ],
        axis=axis,
    )


def gelu_slope(pre):
    return jax.jvp(jax.nn.gelu, (pre,), (jnp.ones_like(pre),))[1]


def hidden_conv(padded, kernel, band_rows):
    lon_cells = padded.shape[2] - 2
    summed = jnp.zeros((padded.shape[0], band_rows, lon_cells, kernel.shape[3]), jnp.float32)
    for row_off in range(3):
        for col_off in range(3):
            summed = summed + jnp.einsum(
                "mrlc,co->mrlo",
                padded[:, row_off : row_off + band_rows, col_off : col_off + lon_cells],
                kernel[row_off, col_off],
                preferred_element_type=jnp.float32,
            )
    return summed


def field_conv(padded, kernel, band_rows):
    lon_cells = padded.shape[2] - 2
    summed = jnp.zeros((padded.shape[0], kernel.shape[3], band_rows, lon_cells), jnp.float32)
    for row_off in range(3):
        for col_off in range(3):
            summed = summed + jnp.einsum(
                "mrlc,cv->mvrl",
                padded[:, row_off : row_off + band_rows, col_off : col_off + lon_cells],
                kernel[row_off, col_off],
                preferred_element_type=jnp.float32,
            )
    return summed


def field_back(padded_grad, kernel, band_rows):
    lon_cells = padded_grad.shape[3] - 2
    summed = jnp.zeros((padded_grad.shape[0], band_rows, lon_cells, kernel.shape[2]), jnp.float32)
    for row_off in range(3):
        for col_off in range(3):
            summed = summed + jnp.einsum(
                "mvrl,cv->mrlc",
                padded_grad[
                    :,
                    :,
                    2 - row_off : 2 - row_off + band_rows,
                    2 - col_off : 2 - col_off + lon_cells,
                ],
                kernel[row_off, col_off],
                preferred_element_type=jnp.float32,
            )
    return summed


def hidden_back(padded_grad, kernel, band_rows):
    lon_cells = padded_grad.shape[2] - 2
    summed = jnp.zeros((padded_grad.shape[0], band_rows, lon_cells, kernel.shape[2]), jnp.float32)
    for row_off in range(3):
        for col_off in range(3):
            summed = summed + jnp.einsum(
                "mrlo,co->mrlc",
                padded_grad[
                    :, 2 - row_off : 2 - row_off + band_rows, 2 - col_off : 2 - col_off + lon_cells
                ],
                kernel[row_off, col_off],
                preferred_element_type=jnp.float32,
            )
    return summed


def kernel_grad(padded_input, grad_out, form, band_rows, lon_cells):
    pieces = []
    for row_off in range(3):
        for col_off in range(3):
            pieces.append(
                jnp.einsum(
                    form,
                    padded_input[:, row_off : row_off + band_rows, col_off : col_off + lon_cells],
                    grad_out,
                    preferred_element_type=jnp.float32,
                )
            )
    return jnp.stack(pieces).reshape((3, 3) + pieces[0].shape)


def pair_sums(own, others, inverse):
    spread = others[None] - own[:, None]
    kernel = jnp.exp(-0.5 * spread * spread * inverse[None, None, :, None, None])
    return jnp.sum(kernel * spread, axis=1)


def member_grad(own, pairwise, truth_piece, inverse, var_weight, members):
    offset = own - truth_piece[None]
    nearness = jnp.exp(-0.5 * offset * offset * inverse[None, :, None, None])
    scale = (var_weight * inverse)[None, :, None, None]
    return scale * (2.0 / (members - 1) * pairwise + 2.0 * nearness * offset)


def split_groups(values, blocks, group):
    shaped = values.reshape((values.shape[0], blocks, group) + values.shape[2:])
    return jnp.moveaxis(shaped, 1, 0)


def shards(features, conv_inner, conv_head, truth, kernel_width, var_weight):
    band_rows = features.shape[1]
    lon_cells = features.shape[2]
    variables = conv_head.shape[3]
    feature_ext = padded_2(features, (("lat", 1),), 1)
    pre_own = hidden_conv(wrap_lon(feature_ext, 2), conv_inner, band_rows)
    hidden_own = jax.nn.gelu(pre_own).astype(jnp.bfloat16)
    hidden_ext = padded_2(hidden_own, (("lat", 1),), 1)
    hidden_wrap = wrap_lon(hidden_ext, 2)
    field = field_conv(hidden_wrap, conv_head, band_rows).astype(jnp.bfloat16)
    inverse = 1.0 / (kernel_width * kernel_width)
    group = 3
    blocks = variables // group
    inverse_blocks = inverse.reshape(blocks, group)
    gathered = lax.all_to_all(field, "mem", split_axis=3, concat_axis=0, tiled=True)
    values = gathered.astype(jnp.float32)
    members = values.shape[0]
    piece_cells = values.shape[3]

    def block_pairs(packed):
        member_values, rates = packed
        return pair_sums(member_values, member_values, rates)

    pairwise = lax.map(block_pairs, (split_groups(values, blocks, group), inverse_blocks))
    pairwise = jnp.moveaxis(pairwise, 0, 1).reshape(values.shape)
    truth_piece = lax.dynamic_slice_in_dim(
        truth, lax.axis_index("mem") * piece_cells, piece_cells, 2
    )
    gradient = member_grad(values, pairwise, truth_piece, inverse, var_weight, members).astype(
        jnp.bfloat16
    )
    field_grad = lax.all_to_all(gradient, "mem", split_axis=0, concat_axis=3, tiled=True)
    grad_pad = padded_2(field_grad, (("lat", 2),), 1)
    hidden_grad = (
        field_back(wrap_lon(grad_pad, 3), conv_head, band_rows) * gelu_slope(pre_own)
    ).astype(jnp.bfloat16)
    head_grad = kernel_grad(hidden_wrap, field_grad, "mrlc,mvrl->cv", band_rows, lon_cells)
    hidden_pad = padded_2(hidden_grad, (("lat", 1),), 1)
    grad_features = hidden_back(wrap_lon(hidden_pad, 2), conv_inner, band_rows).astype(jnp.bfloat16)
    inner_grad = kernel_grad(
        wrap_lon(feature_ext, 2), hidden_grad, "mrlc,mrlo->co", band_rows, lon_cells
    )
    inner_sum, head_sum = lax.psum((inner_grad, head_grad), ("mem", "lat"))
    points = band_rows * lax.axis_size("lat") * lon_cells
    return (grad_features, inner_sum / points, head_sum / points)


def solution(mesh):
    in_specs = (P("mem", "lat", None, None), P(), P(), P(None, "lat", None), P(), P())
    out_specs = (P("mem", "lat", None, None), P(), P())
    return jax.shard_map(shards, mesh=mesh, in_specs=in_specs, out_specs=out_specs, check_vma=False)
```

profile of v0, /device:TPU:1, one launch (start us, length us, event | category | flops | bytes accessed | tf_op | source)
XLA Modules:
  0.0 686.9 jit_solution(1620090667409105720)
XLA Ops:
  9.4 4.6 collective-permute-start
  19.4 10.9 %collective-permute-done = bf16[4,1,1440,128]{3,2,1,0:T(8,128)(2,1)S(1)} collective-permute-done((bf16[4,1,1440,128]{3,2,1,0:T(8,128)(2,1)S(1)}, bf16[4,1,1440,128]{3,2,1,0:T(8,128)(2,1)S(1)}, u32[]{:S(2)}, u32[]{:S(2)}) %collective-permute-start) | collective-permute-done | bytes 1474592 | tf_op jit(solution)/shard_map/ppermute | solution.py:15
  59.7 21.2 %multiply_convert_fusion = (bf16[4,2,1440,128]{3,2,1,0:T(8,128)(2,1)}, f32[4,2,1440,128]{3,2,1,0:T(8,128)}) fusion(bf16[3,3,128,128]{3,2,1,0:T(8,128)(2,1)S(1)} %copy-done.21, bf16[4,4,1,128]{3,2,1,0:T(2,128)(2,1)S(1)} %get-tuple-element.58, bf16[4,4,1440,128]{3,2,1,0:T(8,128)(2,1)} %copy-done.2, f32[4,2,1440,128]{3,2,1,0:T(8,128)} %fusion.168, ...), kind=kOutput, calls=%fused_computation.42 | convolution fusion | flops 408453120 | bytes 61972480 | tf_op jit(solution)/shard_map/mrlc,co->mrlo/dot_general | solution.py:45
  90.1 12.3 %collective-permute-done.2 = bf16[4,1,1440,128]{3,2,1,0:T(8,128)(2,1)S(1)} collective-permute-done((bf16[4,1,1440,128]{3,2,1,0:T(8,128)(2,1)S(1)}, bf16[4,1,1440,128]{3,2,1,0:T(8,128)(2,1)S(1)}, u32[]{:S(2)}, u32[]{:S(2)}) %collective-permute-start.2) | collective-permute-done | bytes 1474592 | tf_op jit(solution)/shard_map/ppermute | solution.py:15
  102.4 4.4 collective-permute-done.3
  106.8 7.3 %fusion.7 = (bf16[4,4,1441,128]{3,2,1,0:T(8,128)(2,1)S(1)}, bf16[4,4,1441,128]{3,2,1,0:T(8,128)(2,1)S(1)}) fusion(bf16[4,1,1440,128]{3,2,1,0:T(8,128)(2,1)S(1)} %collective-permute-done.3, bf16[4,2,1440,128]{3,2,1,0:T(8,128)(2,1)S(1)} %copy-done.5, bf16[4,1,1440,128]{3,2,1,0:T(8,128)(2,1)S(1)} %collective-permute-done.2), kind=kLoop, calls=%fused_computation.27 | loop fusion | flops 70828032 | bytes 17702912 | tf_op jit(solution)/shard_map/concatenate | solution.py:26
  136.3 8.5 %fusion.71 = bf16[4,69,2,1440]{3,1,2,0:T(8,128)(2,1)} fusion(bf16[4,4,1441,128]{3,2,1,0:T(8,128)(2,1)S(1)} %get-tuple-element.57, f32[4,2,1440,69]{2,3,1,0:T(8,128)S(1)} %fusion.53, f32[4,2,1440,69]{2,3,1,0:T(8,128)} %fusion.76, f32[4,2,1440,69]{2,3,1,0:T(8,128)} %fusion.80, f32[4,2,1440,69]{2,3,1,0:T(8,128)S(1)} %fusion.218, ...), kind=kOutput, calls=%fused_computation.109 | convolution fusion | flops 210643200 | bytes 31071744 | tf_op jit(solution)/shard_map/mrlc,cv->mvrl/dot_general | solution.py:59
  144.8 8.4 %copy.54 = bf16[4,69,2,1440]{1,2,0,3:T(2,128)(2,1)} copy(bf16[4,69,2,1440]{3,1,2,0:T(8,128)(2,1)} %fusion.71) | data formatting | bytes 3179520 | tf_op jit(solution)/shard_map/convert_element_type | solution.py:145
  153.2 7.5 %all-to-all-start = ((bf16[4,69,2,1440]{1,2,0,3:T(2,128)(2,1)}), bf16[4,69,2,1440]{1,2,0,3:T(2,128)(2,1)}, u32[]{:S(2)}, u32[]{:S(2)}) async-start(bf16[4,69,2,1440]{1,2,0,3:T(2,128)(2,1)} %copy.54), calls=%async_computation | async-start | bytes 5898240 | tf_op jit(solution)/shard_map/all_to_all | solution.py:150
  161.1 23.6 %all-to-all-done = bf16[4,69,2,1440]{1,2,0,3:T(2,128)(2,1)} async-done(((bf16[4,69,2,1440]{1,2,0,3:T(2,128)(2,1)}), bf16[4,69,2,1440]{1,2,0,3:T(2,128)(2,1)}, u32[]{:S(2)}, u32[]{:S(2)}) %all-to-all-start) | async-done | bytes 1589792 | tf_op jit(solution)/shard_map/all_to_all | solution.py:150
  184.7 7.7 %copy.55 = bf16[4,69,2,1440]{3,0,2,1:T(4,128)(2,1)S(1)} copy(bf16[4,69,2,1440]{1,2,0,3:T(2,128)(2,1)} %all-to-all-done) | data formatting | bytes 3179520 | tf_op jit(solution)/shard_map/all_to_all | solution.py:150
  194.8 6.2 reshape.41
  201.0 6.8 copy.57
  211.3 91.5 %while.10 = (s32[]{:T(128)}, f32[23,32,3,2,180]{4,1,3,2,0:T(8,128)}, f32[23,32,3,2,180]{4,3,2,0,1:T(2,128)}, f32[23,3]{1,0:T(8,128)S(1)}, s32[]{:T(128)}) while((s32[]{:T(128)}, f32[23,32,3,2,180]{4,1,3,2,0:T(8,128)}, f32[23,32,3,2,180]{4,3,2,0,1:T(2,128)}, f32[23,3]{1,0:T(8,128)S(1)}, s32[]{:T(128)}) %tuple.48), condition=%wide.region_2.3_spmd, body=%wide.region_0.2_spmd.sunk | while | flops 6600962 | bytes 1302645 | solution.py:159
  306.5 6.4 fusion.26
  315.2 22.8 %all_to_all.27 = bf16[32,69,2,180]{3,2,1,0:T(2,128)(2,1)S(1)} all-to-all(bf16[32,69,2,180]{3,2,1,0:T(2,128)(2,1)S(1)} %copy.62), channel_id=1, replica_groups=mesh['mem'=8,'lat'=16] {'mem'}, dimensions={0} | all-to-all | bytes 3179520 | tf_op jit(solution)/shard_map/all_to_all | solution.py:167
  357.0 27.5 %collective-permute-start.4 = (bf16[4,69,1,1440]{3,0,2,1:T(4,128)(2,1)S(1)}, bf16[4,69,1,1440]{3,0,2,1:T(4,128)(2,1)S(1)}, u32[]{:S(2)}, u32[]{:S(2)}) collective-permute-start(bf16[4,69,1,1440]{3,0,2,1:T(4,128)(2,1)S(1)} %copy.65), channel_id=1, source_target_pairs={{0,1},{1,2},{2,3},{3,4},{4,5},{5,6},{6,7},{7,8},{8,9},{9,10},{10,1... | collective-permute-start | bytes 2384648 | tf_op jit(solution)/shard_map/ppermute | solution.py:15
  403.1 4.2 fusion.95
  427.3 21.4 %fusion.19 = bf16[4,2,1440,128]{3,2,1,0:T(8,128)(2,1)} fusion(f32[4,2,1440,128]{3,2,1,0:T(8,128)} %get-tuple-element.82, f32[4,2,1440,128]{3,2,1,0:T(8,128)} %fusion.61, f32[4,2,1440,128]{3,2,1,0:T(8,128)} %fusion.108, f32[4,2,1440,128]{3,2,1,0:T(8,128)} %fusion.95, f32[4,2,1440,128]{3,2,1,0:T(8,128)} %fusion.216, f32[4,2,1440,128]{3,2,1,0:T(8,128)} %fusion.101, ...), kind=kOutput, calls=%fused_computation.40 | convolution fusion | flops 245007360 | bytes 59526144 | tf_op jit(solution)/shard_map/mvrl,cv->mrlc/dot_general | solution.py:73
  472.0 5.3 fusion.175
  477.3 145.3 %all-reduce.3.cloned.1.call-done = (f32[3,3,128,128]{3,2,1,0:T(8,128)}, f32[3,3,128,69]{2,3,1,0:T(8,128)}) async-done(((f32[3,3,128,128]{3,2,1,0:T(8,128)}, f32[3,3,128,69]{2,3,1,0:T(8,128)}), (f32[3,3,128,128]{3,2,1,0:T(8,128)}, f32[3,3,128,69]{2,3,1,0:T(8,128)})) %all-reduce.3.cloned.1.call-update) | async-done | bytes 907792 | tf_op jit(solution)/shard_map/psum | solution.py:178
  626.2 7.7 %fusion.4 = (bf16[4,4,1441,128]{3,2,1,0:T(8,128)(2,1)S(1)}, bf16[4,4,1441,128]{3,2,1,0:T(8,128)(2,1)S(1)}) fusion(bf16[4,1,1440,128]{3,2,1,0:T(8,128)(2,1)S(1)} %collective-permute-done.7, bf16[4,2,1440,128]{3,2,1,0:T(8,128)(2,1)} %fusion.19, bf16[4,1,1440,128]{3,2,1,0:T(8,128)(2,1)} %collective-permute-done.6), kind=kLoop, calls=%fused_computation.18 | loop fusion | flops 70828032 | bytes 17702912 | tf_op jit(solution)/shard_map/concatenate | solution.py:26
  652.2 4.8 fusion.31
  660.4 19.4 %add_convert_fusion = bf16[4,2,1440,128]{3,2,1,0:T(8,128)(2,1)} fusion(f32[4,2,1440,128]{3,2,1,0:T(8,128)} %fusion.31, f32[4,2,1440,128]{3,2,1,0:T(8,128)} %fusion.43, f32[4,2,1440,128]{3,2,1,0:T(8,128)} %fusion.45, f32[4,2,1440,128]{3,2,1,0:T(8,128)} %fusion.175, f32[4,2,1440,128]{3,2,1,0:T(8,128)} %fusion.47, f32[4,2,1440,128]{3,2,1,0:T(8,128)} %fusion.49, ...), kind=kOutput, calls=%fused_computation.41 | convolution fusion | flops 390758400 | bytes 53116928 | tf_op jit(solution)/shard_map/mrlo,co->mrlc/dot_general | solution.py:92
  (282 shorter events, 277.6 us)
Async XLA Ops:
  7.2 153.7 %copy-start = (f32[69,2,1440]{2,1,0:T(2,128)S(1)}, f32[69,2,1440]{2,1,0:T(2,128)}, u32[]{:S(2)}) copy-start(f32[69,2,1440]{2,1,0:T(2,128)} %param.11) | copy-start | bytes 2384644
  9.4 20.9 %collective-permute-start = (bf16[4,1,1440,128]{3,2,1,0:T(8,128)(2,1)S(1)}, bf16[4,1,1440,128]{3,2,1,0:T(8,128)(2,1)S(1)}, u32[]{:S(2)}, u32[]{:S(2)}) collective-permute-start(bf16[4,1,1440,128]{3,2,1,0:T(8,128)(2,1)S(1)} %get-tuple-element.69), channel_id=1, source_target_pairs={{0,1},{1,2},{2,3},{3,4},{4,5},{5,6},{6,7},{7,8},{8,9},{9,10},{10,1... | collective-permute-start | bytes 4423688 | tf_op jit(solution)/shard_map/ppermute | solution.py:15
  14.0 20.7 %collective-permute-start.1 = (bf16[4,1,1440,128]{3,2,1,0:T(8,128)(2,1)S(1)}, bf16[4,1,1440,128]{3,2,1,0:T(8,128)(2,1)S(1)}, u32[]{:S(2)}, u32[]{:S(2)}) collective-permute-start(bf16[4,1,1440,128]{3,2,1,0:T(8,128)(2,1)S(1)} %get-tuple-element.70), channel_id=1, source_target_pairs={{1,0},{2,1},{3,2},{4,3},{5,4},{6,5},{7,6},{8,7},{9,8},{10,9},{11,1... | collective-permute-start | bytes 4423688 | tf_op jit(solution)/shard_map/ppermute | solution.py:17
  32.5 23.8 %copy-start.15 = (bf16[4,3,1440,128]{3,2,1,0:T(8,128)(2,1)}, bf16[4,3,1440,128]{3,2,1,0:T(8,128)(2,1)S(1)}, u32[]{:S(2)}) copy-start(bf16[4,3,1440,128]{3,2,1,0:T(8,128)(2,1)S(1)} %get-tuple-element.66) | copy-start | bytes 13271044
  35.2 14.3 %copy-start.2 = (bf16[4,4,1440,128]{3,2,1,0:T(8,128)(2,1)}, bf16[4,4,1440,128]{3,2,1,0:T(8,128)(2,1)S(1)}, u32[]{:S(2)}) copy-start(bf16[4,4,1440,128]{3,2,1,0:T(8,128)(2,1)S(1)} %get-tuple-element.75) | copy-start | bytes 17694724
  35.2 17.7 %copy-start.14 = (bf16[4,3,1440,128]{3,2,1,0:T(8,128)(2,1)}, bf16[4,3,1440,128]{3,2,1,0:T(8,128)(2,1)S(1)}, u32[]{:S(2)}) copy-start(bf16[4,3,1440,128]{3,2,1,0:T(8,128)(2,1)S(1)} %get-tuple-element.76) | copy-start | bytes 13271044
  35.3 14.2 %copy-start.26 = (bf16[4,4,1,128]{3,2,1,0:T(2,128)(2,1)}, bf16[4,4,1,128]{3,2,1,0:T(2,128)(2,1)S(1)}, u32[]{:S(2)}) copy-start(bf16[4,4,1,128]{3,2,1,0:T(2,128)(2,1)S(1)} %get-tuple-element.59) | copy-start | bytes 12292
  83.1 19.3 %collective-permute-start.2 = (bf16[4,1,1440,128]{3,2,1,0:T(8,128)(2,1)S(1)}, bf16[4,1,1440,128]{3,2,1,0:T(8,128)(2,1)S(1)}, u32[]{:S(2)}, u32[]{:S(2)}) collective-permute-start(bf16[4,1,1440,128]{3,2,1,0:T(8,128)(2,1)S(1)} %get-tuple-element.64), channel_id=1, source_target_pairs={{0,1},{1,2},{2,3},{3,4},{4,5},{5,6},{6,7},{7,8},{8,9},{9,10},{10,1... | collective-permute-start | bytes 4423688 | tf_op jit(solution)/shard_map/ppermute | solution.py:15
  86.1 20.7 %collective-permute-start.3 = (bf16[4,1,1440,128]{3,2,1,0:T(8,128)(2,1)S(1)}, bf16[4,1,1440,128]{3,2,1,0:T(8,128)(2,1)S(1)}, u32[]{:S(2)}, u32[]{:S(2)}) collective-permute-start(bf16[4,1,1440,128]{3,2,1,0:T(8,128)(2,1)S(1)} %get-tuple-element.65), channel_id=1, source_target_pairs={{1,0},{2,1},{3,2},{4,3},{5,4},{6,5},{7,6},{8,7},{9,8},{10,9},{11,1... | collective-permute-start | bytes 4423688 | tf_op jit(solution)/shard_map/ppermute | solution.py:17
  102.4 32.1 %copy-start.19 = (bf16[4,1,1440,128]{3,2,1,0:T(8,128)(2,1)}, bf16[4,1,1440,128]{3,2,1,0:T(8,128)(2,1)S(1)}, u32[]{:S(2)}) copy-start(bf16[4,1,1440,128]{3,2,1,0:T(8,128)(2,1)S(1)} %collective-permute-done.2) | copy-start | bytes 4423684
  106.8 25.9 %copy-start.17 = (bf16[4,1,1440,128]{3,2,1,0:T(8,128)(2,1)}, bf16[4,1,1440,128]{3,2,1,0:T(8,128)(2,1)S(1)}, u32[]{:S(2)}) copy-start(bf16[4,1,1440,128]{3,2,1,0:T(8,128)(2,1)S(1)} %collective-permute-done.3) | copy-start | bytes 4423684
  114.1 22.2 %copy-start.11 = (bf16[4,4,1441,128]{3,2,1,0:T(8,128)(2,1)}, bf16[4,4,1441,128]{3,2,1,0:T(8,128)(2,1)S(1)}, u32[]{:S(2)}) copy-start(bf16[4,4,1441,128]{3,2,1,0:T(8,128)(2,1)S(1)} %get-tuple-element.57) | copy-start | bytes 17707012
  144.8 16.0 %copy-start.28 = (f32[69]{0:T(128)S(1)}, f32[69]{0:T(128)}, u32[]{:S(2)}) copy-start(f32[69]{0:T(128)} %param.13) | copy-start | bytes 832
  144.8 16.0 %copy-start.29 = (f32[69]{0:T(128)S(1)}, f32[69]{0:T(128)}, u32[]{:S(2)}) copy-start(f32[69]{0:T(128)} %param.12) | copy-start | bytes 832
  153.2 31.5 %all-to-all-start = ((bf16[4,69,2,1440]{1,2,0,3:T(2,128)(2,1)}), bf16[4,69,2,1440]{1,2,0,3:T(2,128)(2,1)}, u32[]{:S(2)}, u32[]{:S(2)}) async-start(bf16[4,69,2,1440]{1,2,0,3:T(2,128)(2,1)} %copy.54), calls=%async_computation | async-start | bytes 5898240 | tf_op jit(solution)/shard_map/all_to_all | solution.py:150
  160.7 461.8 %all-reduce.3.cloned.1.call-start = ((), (), s32[]{:S(2)}) async-start(), calls=%async_computation.2 | async-start | bytes 1843200 | tf_op jit(solution)/shard_map/psum | solution.py:178
  355.4 31.3 %copy-start.18 = (bf16[4,1,1440,128]{3,2,1,0:T(8,128)(2,1)S(1)}, bf16[4,1,1440,128]{3,2,1,0:T(8,128)(2,1)}, u32[]{:S(2)}) copy-start(bf16[4,1,1440,128]{3,2,1,0:T(8,128)(2,1)} %copy-done.17) | copy-start | bytes 4423684
  357.0 37.1 %collective-permute-start.4 = (bf16[4,69,1,1440]{3,0,2,1:T(4,128)(2,1)S(1)}, bf16[4,69,1,1440]{3,0,2,1:T(4,128)(2,1)S(1)}, u32[]{:S(2)}, u32[]{:S(2)}) collective-permute-start(bf16[4,69,1,1440]{3,0,2,1:T(4,128)(2,1)S(1)} %copy.65), channel_id=1, source_target_pairs={{0,1},{1,2},{2,3},{3,4},{4,5},{5,6},{6,7},{7,8},{8,9},{9,10},{10,1... | collective-permute-start | bytes 2384648 | tf_op jit(solution)/shard_map/ppermute | solution.py:15
  384.5 14.0 %collective-permute-start.5 = (bf16[4,69,1,1440]{3,0,2,1:T(4,128)(2,1)S(1)}, bf16[4,69,1,1440]{3,0,2,1:T(4,128)(2,1)S(1)}, u32[]{:S(2)}, u32[]{:S(2)}) collective-permute-start(bf16[4,69,1,1440]{3,0,2,1:T(4,128)(2,1)S(1)} %copy.66), channel_id=1, source_target_pairs={{1,0},{2,1},{3,2},{4,3},{5,4},{6,5},{7,6},{8,7},{9,8},{10,9},{11,1... | collective-permute-start | bytes 2384648 | tf_op jit(solution)/shard_map/ppermute | solution.py:17
  398.7 16.8 %copy-start.7 = (bf16[4,69,4,1440]{3,1,2,0:T(8,128)(2,1)}, bf16[4,69,4,1440]{3,1,2,0:T(8,128)(2,1)S(1)}, u32[]{:S(2)}) copy-start(bf16[4,69,4,1440]{3,1,2,0:T(8,128)(2,1)S(1)} %get-tuple-element.78) | copy-start | bytes 9538564
  427.3 21.4 %copy-start.27 = (bf16[4,4,1,128]{3,2,1,0:T(2,128)(2,1)S(1)}, bf16[4,4,1,128]{3,2,1,0:T(2,128)(2,1)}, u32[]{:S(2)}) copy-start(bf16[4,4,1,128]{3,2,1,0:T(2,128)(2,1)} %copy-done.26) | copy-start | bytes 12292
  463.3 162.9 %collective-permute-start.7 = (bf16[4,1,1440,128]{3,2,1,0:T(8,128)(2,1)}, bf16[4,1,1440,128]{3,2,1,0:T(8,128)(2,1)S(1)}, u32[]{:S(2)}, u32[]{:S(2)}) collective-permute-start(bf16[4,1,1440,128]{3,2,1,0:T(8,128)(2,1)} %get-tuple-element.62), channel_id=1, source_target_pairs={{1,0},{2,1},{3,2},{4,3},{5,4},{6,5},{7,6},{8,7},{9,8},{10,9},{11,1... | collective-permute-start | bytes 4423688 | tf_op jit(solution)/shard_map/ppermute | solution.py:17
  465.3 161.0 %collective-permute-start.6 = (bf16[4,1,1440,128]{3,2,1,0:T(8,128)(2,1)}, bf16[4,1,1440,128]{3,2,1,0:T(8,128)(2,1)}, u32[]{:S(2)}, u32[]{:S(2)}) collective-permute-start(bf16[4,1,1440,128]{3,2,1,0:T(8,128)(2,1)} %get-tuple-element.63), channel_id=1, source_target_pairs={{0,1},{1,2},{2,3},{3,4},{4,5},{5,6},{6,7},{7,8},{8,9},{9,10},{10,1... | collective-permute-start | bytes 4423688 | tf_op jit(solution)/shard_map/ppermute | solution.py:15
  660.4 19.4 %copy-start.1 = (f32[69,2,1440]{2,1,0:T(2,128)S(1)}, f32[69,2,1440]{2,1,0:T(2,128)}, u32[]{:S(2)}) copy-start(f32[69,2,1440]{2,1,0:T(2,128)} %param.11) | copy-start | bytes 2384644
  (24 other events, 118.1 us)
Sparse Core Ops, SparseCore 0:
  472.1 150.3 all-reduce.2
where the time goes:
time: 698 us; the launch traced here: 687 us
  matrix products  210 us (30%)
  waiting for transfers between devices  204 us (29%)
  local copies, waits for them, and re-layouts  98.7 us (14%)
  other arithmetic  81.2 us (12%)
  starting transfers between devices  54.5 us (8%)
  blocking collectives  22.8 us (3%)
  between operations  15 us (2%)
    psum x1, waiting for transfers between devices, shards(): inner_sum, head_sum = lax.psum((inner_grad, head_grad), ('mem', 'lat'))  145 us
    dot_general x9, matrix products, field_back(): jnp.einsum('mvrl,cv->mrlc', padded_grad[:, :, 2 - row_off:2 - row_off + b...  53.3 us
    reduce_sum x23, other arithmetic, pair_sums(): return jnp.sum(kernel * spread, axis=1)  52.8 us
    dot_general x9, matrix products, hidden_back(): jnp.einsum('mrlo,co->mrlc', padded_grad[:, 2 - row_off:2 - row_off + band...  50.8 us
    dot_general x9, matrix products, hidden_conv(): jnp.einsum('mrlc,co->mrlo', padded[:, row_off:row_off + band_rows, col_of...  49.1 us
    ppermute x4, starting transfers between devices, padded_2(): lax.ppermute(tail, axis, [(i, (i + 1) % count) for i in range(ends)])  38.9 us
    dot_general x9, matrix products, field_conv(): jnp.einsum('mrlc,cv->mvrl', padded[:, row_off:row_off + band_rows, col_of...  32.5 us
    ppermute x4, waiting for transfers between devices, padded_2(): lax.ppermute(tail, axis, [(i, (i + 1) % count) for i in range(ends)])  25 us
  transfers between devices with their start and end apart: 10, of which 8 were waited for; matrix products, arithmetic and copies ran while one was open for 4% of the time, Pallas kernels for 0%

commit v1 on v0

v1 whole, which is shorter than its diff:
```python
import math
import jax
import jax.numpy as jnp
from jax import lax
from jax.experimental import pallas as pl
from jax.experimental.pallas import tpu as pltpu
from jax.sharding import PartitionSpec as P

MESH_ID = pl.DeviceIdType.MESH
F32 = jnp.float32
BF16 = jnp.bfloat16
LANE = 128
VP = 80
MEM = 8
LAT = 16
GELU_A = math.sqrt(2.0 / math.pi)
GELU_B = 0.044715


def roll_rows(values, shift):
    return pltpu.roll(values, shift % values.shape[0], 0)


def transposed(values):
    return jnp.transpose(values.astype(F32)).astype(BF16)


def whole_block(
    feat, kin, ht, prm, truth,
    gf_out, gi_out, gh_out,
    feat_rows, wide, shifted, slope, hgrad, hgrad_t, own_field,
    part_out, part_in, field_out, values_in, grad_field,
    w_inner, w_head, w_head_back, w_inner_back,
    inner_acc, head_acc, ar_in, ar_out, ar_r1, ar_r2, ar_r3, gf_buf,
    load_sem, fh_s, fh_r, ph_s, ph_r, a2_s, a2_r, b2_s, b2_r, gh_s, gh_r, hh_s, hh_r,
    r1_s, r1_r, r2_s, r2_r, r3_s, r3_r, g3_s, g3_r, g2_s, g2_r, g1_s, g1_r, out_sem,
):
    lon = feat.shape[2]
    lon_pad = grad_field.shape[3]
    members = feat.shape[0]
    third = lon_pad // 4
    d = lax.axis_index("mem")
    r = lax.axis_index("lat")
    has_up = r > 0
    has_down = r < LAT - 1
    above = lax.rem(r + LAT - 1, LAT)
    below = lax.rem(r + 1, LAT)
    half = lax.rem(r, 2)
    seat = r // 2

    def mem_peer(k):
        return lax.rem(d + k, MEM)

    def lat_peer(k):
        return lax.rem(seat + k, MEM) * 2 + half

    partner = r + 1 - 2 * half

    def remote(src, dst, ss, rs, **where):
        return pltpu.make_async_remote_copy(
            src_ref=src, dst_ref=dst, send_sem=ss, recv_sem=rs,
            device_id=where, device_id_type=MESH_ID,
        )

    barrier = pltpu.get_barrier_semaphore()
    for k in range(1, MEM):
        pl.semaphore_signal(barrier, inc=1, device_id={"mem": mem_peer(k)}, device_id_type=MESH_ID)
    for k in range(1, LAT):
        pl.semaphore_signal(
            barrier, inc=1, device_id={"lat": lax.rem(r + k, LAT)}, device_id_type=MESH_ID
        )

    def load(m, row):
        return pltpu.make_async_copy(
            feat.at[m, row], feat_rows.at[1 + row, m, pl.ds(0, lon)], load_sem.at[m, row]
        )

    for m in range(members):
        for row in range(2):
            load(m, row).start()

    pl.semaphore_wait(barrier, MEM - 1 + LAT - 1)

    def feat_halo(side, m):
        if side == 0:
            src, dst, where = feat_rows.at[1, m, pl.ds(0, lon)], feat_rows.at[3, m, pl.ds(0, lon)], above
        else:
            src, dst, where = feat_rows.at[2, m, pl.ds(0, lon)], feat_rows.at[0, m, pl.ds(0, lon)], below
        return remote(src, dst, fh_s.at[side, m], fh_r.at[side, m], lat=where)

    def part_halo(side, m):
        src = part_out.at[pl.ds(side * 4, 4), m]
        dst = part_in.at[pl.ds(side * 4, 4), m]
        return remote(src, dst, ph_s.at[side, m], ph_r.at[side, m], lat=above if side == 0 else below)

    def gfield_halo(side, m):
        if side == 0:
            src, dst, where = grad_field.at[m, 1], grad_field.at[m, 3], above
        else:
            src, dst, where = grad_field.at[m, 2], grad_field.at[m, 0], below
        return remote(src, dst, gh_s.at[side, m], gh_r.at[side, m], lat=where)

    def hgrad_halo(side, m):
        if side == 0:
            src, dst, where = hgrad.at[1, m], hgrad.at[3, m], above
        else:
            src, dst, where = hgrad.at[2, m], hgrad.at[0, m], below
        return remote(src, dst, hh_s.at[side, m], hh_r.at[side, m], lat=where)

    sides = ((0, has_up, has_down), (1, has_down, has_up))

    def send_halo(copy_of, m):
        for side, sends, _ in sides:
            @pl.when(sends)
            def _():
                copy_of(side, m).start()

    def recv_halo(copy_of, m):
        for side, _, receives in sides:
            @pl.when(receives)
            def _():
                copy_of(side, m).wait_recv()

    def drain_halo(copy_of, m):
        for side, sends, _ in sides:
            @pl.when(sends)
            def _():
                copy_of(side, m).wait_send()

    for m in range(members):
        for row in range(2):
            load(m, row).wait()
        send_halo(feat_halo, m)

    feat_rows[:, :, lon:, :] = jnp.zeros((4, members, lon_pad - lon, LANE), BF16)
    shifted[:, lon:, :] = jnp.zeros((members, lon_pad - lon, shifted.shape[2]), BF16)

    @pl.when(r == 0)
    def _():
        for m in range(members):
            feat_rows[0, m, 0:lon] = jnp.zeros((lon, LANE), BF16)
            hgrad[0, m] = jnp.zeros((lon, LANE), BF16)
            grad_field[m, 0] = jnp.zeros((VP, lon_pad), BF16)
            for q in range(4):
                part_in[4 + q, m] = jnp.zeros((VP, third), BF16)

    @pl.when(r == LAT - 1)
    def _():
        for m in range(members):
            feat_rows[3, m, 0:lon] = jnp.zeros((lon, LANE), BF16)
            hgrad[3, m] = jnp.zeros((lon, LANE), BF16)
            grad_field[m, 3] = jnp.zeros((VP, lon_pad), BF16)
            for q in range(4):
                part_in[q, m] = jnp.zeros((VP, third), BF16)

    w_inner[...] = jnp.zeros(w_inner.shape, BF16)
    w_inner_back[...] = jnp.zeros(w_inner_back.shape, BF16)
    w_head[...] = jnp.zeros(w_head.shape, BF16)
    w_head_back[...] = jnp.zeros(w_head_back.shape, BF16)
    for a in range(3):
        for b in range(3):
            block = kin[a * 3 + b]
            block_t = transposed(block)
            head_t = ht[a * 3 + b]
            for o in range(2):
                cols = slice((o * 3 + b) * LANE, (o * 3 + b + 1) * LANE)
                w_inner[(o + a) * LANE:(o + a + 1) * LANE, cols] = block
                e = o - a + 2
                w_inner_back[e * LANE:(e + 1) * LANE, cols] = block_t
                row = o - a + 2
                w_head[row * VP:(row + 1) * VP, b * 2 * LANE + o * LANE:b * 2 * LANE + (o + 1) * LANE] = head_t
            w_head_back[(2 - a) * VP:(3 - a) * VP, b * LANE:(b + 1) * LANE] = head_t

    def lanes(index):
        return slice(index * LANE, (index + 1) * LANE)

    def forward(m):
        recv_halo(feat_halo, m)
        rows = jnp.concatenate([feat_rows[e, m, 0:lon] for e in range(4)], axis=1)
        wide[...] = jnp.dot(rows, w_inner[...], preferred_element_type=F32)
        for o in range(2):
            pre = (
                roll_rows(wide[:, lanes(o * 3)], 1)
                + wide[:, lanes(o * 3 + 1)]
                + roll_rows(wide[:, lanes(o * 3 + 2)], -1)
            )
            square = pre * pre
            th = jnp.tanh(GELU_A * pre * (1.0 + GELU_B * square))
            cdf = 0.5 + 0.5 * th
            hidden = pre * cdf
            grad = cdf + 0.5 * pre * (1.0 - th * th) * (GELU_A * (1.0 + 3.0 * GELU_B * square))
            slope[m, :, lanes(o)] = grad.astype(BF16)
            shifted[m, 0:lon, lanes(o)] = roll_rows(hidden, 1).astype(BF16)
            shifted[m, 0:lon, lanes(2 + o)] = hidden.astype(BF16)
            shifted[m, 0:lon, lanes(4 + o)] = roll_rows(hidden, -1).astype(BF16)
        slot = lax.rem(m, 2)
        for q in range(4):
            sums = lax.dot_general(
                w_head[...], shifted[m, q * third:(q + 1) * third, :],
                (((1,), (1,)), ((), ())), preferred_element_type=F32,
            )
            part_out[q, m] = sums[0:VP].astype(BF16)
            own_field[slot, 0, :, q * third:(q + 1) * third] = sums[VP:2 * VP]
            own_field[slot, 1, :, q * third:(q + 1) * third] = sums[2 * VP:3 * VP]
            part_out[4 + q, m] = sums[3 * VP:4 * VP].astype(BF16)
        send_halo(part_halo, m)

    def field_copy(m, k):
        p = mem_peer(k)
        return remote(
            field_out.at[p, m], values_in.at[d, m], a2_s.at[m, k], a2_r.at[m, k], mem=p
        )

    def finish_field(m):
        recv_halo(part_halo, m)
        slot = lax.rem(m, 2)
        for row in range(2):
            for q in range(4):
                total = own_field[slot, row, :, q * third:(q + 1) * third] + part_in[
                    (1 - row) * 4 + q, m
                ].astype(F32)
                field_out[row * 4 + q, m] = total.astype(BF16)
        for k in range(1, MEM):
            field_copy(m, k).start()
        values_in[d, m] = field_out[d, m]

    def forward_step(step, carry):
        @pl.when(step < members)
        def _():
            forward(step)

        @pl.when(step > 0)
        def _():
            finish_field(step - 1)

        return carry

    lax.fori_loop(0, members + 1, forward_step, 0)

    def wait_fields(m, carry):
        for k in range(1, MEM):
            field_copy(m, k).wait()
        drain_halo(feat_halo, m)
        drain_halo(part_halo, m)
        return carry

    lax.fori_loop(0, members, wait_fields, 0)

    grad_out = field_out
    count = MEM * members
    own_row = 1 + d // 4
    own_lane = lax.rem(d, 4) * third

    def place(j):
        return slice((j // 6) * VP, (j // 6 + 1) * VP), slice((j % 6) * LANE, (j % 6 + 1) * LANE)

    def back_copy(c, k):
        p = mem_peer(k)
        return remote(
            grad_out.at[p, :, :, pl.ds(c * LANE, LANE)],
            grad_field.at[:, own_row, :, pl.ds(own_lane + c * LANE, LANE)],
            b2_s.at[c, k], b2_r.at[c, k], mem=p,
        )

    block = 8

    def pair_chunk(c, carry):
        lane = pl.ds(pl.multiple_of(c * LANE, LANE), LANE)
        scale = prm[0]
        for j in range(count):
            rows, cols = place(j)
            wide[rows, cols] = values_in[j // members, j % members, :, lane].astype(F32) * scale

        def group(g, inner):
            def at(j):
                base = (j // 6) * VP
                return pl.ds(pl.multiple_of(base + g * 8, 8), 8), slice((j % 6) * LANE, (j % 6 + 1) * LANE)

            rows8 = pl.ds(pl.multiple_of(g * 8, 8), 8)
            target = truth[rows8, lane] * prm[0, rows8]
            pair_weight = prm[1, rows8]
            truth_weight = prm[2, rows8]

            def term(x, y):
                u = x - y
                return u * jnp.exp2(u * (y - x))

            for i0 in range(0, count, block):
                xi = [wide[at(i0 + i)] for i in range(block)]
                sums = [None] * block
                for i in range(block):
                    for j in range(i + 1, block):
                        w = term(xi[j], xi[i])
                        sums[i] = w if sums[i] is None else sums[i] + w
                        sums[j] = -w if sums[j] is None else sums[j] - w
                if i0 > 0:
                    sums = [s + wide[at(count + i0 + i)] for i, s in enumerate(sums)]
                for j0 in range(i0 + block, count, 4):
                    xj = [wide[at(j0 + j)] for j in range(4)]
                    back = [None] * 4
                    for j in range(4):
                        for i in range(block):
                            w = term(xj[j], xi[i])
                            sums[i] = sums[i] + w
                            back[j] = -w if back[j] is None else back[j] - w
                    for j in range(4):
                        old = back[j] if i0 == 0 else wide[at(count + j0 + j)] + back[j]
                        wide[at(count + j0 + j)] = old
                for i in range(block):
                    near = term(xi[i], target)
                    wide[at(count + i0 + i)] = pair_weight * sums[i] + truth_weight * near
            return inner

        lax.fori_loop(0, VP // 8 - 1, group, 0)
        pad_row = jnp.zeros((VP - 72, LANE), F32)
        for j in range(count):
            rows, cols = place(count + j)
            full = jnp.concatenate([wide[rows, cols][0:72], pad_row], axis=0)
            grad_out[j // members, j % members, :, lane] = full.astype(BF16)
        for k in range(1, MEM):
            back_copy(c, k).start()
        grad_field[:, own_row, :, pl.ds(pl.multiple_of(own_lane + c * LANE, LANE), LANE)] = grad_out[d, :, :, lane]
        return carry

    chunks = third // LANE
    lax.fori_loop(0, chunks, pair_chunk, 0)

    def wait_back(c, carry):
        for k in range(1, MEM):
            back_copy(c, k).wait()
        return carry

    lax.fori_loop(0, chunks, wait_back, 0)

    for m in range(members):
        send_halo(gfield_halo, m)

    inner_acc[...] = jnp.zeros(inner_acc.shape, F32)
    head_acc[...] = jnp.zeros(head_acc.shape, F32)

    def backward(m, carry):
        recv_halo(gfield_halo, m)
        for i in range(2):
            stack = [grad_field[m, i + j] for j in range(3)]
            stack.append(jnp.zeros((2 * LANE - 3 * VP, lon_pad), BF16))
            columns = transposed(jnp.concatenate(stack, axis=0))
            wide[:, 0:3 * LANE] = jnp.dot(
                columns[0:lon], w_head_back[...], preferred_element_type=F32
            )
            total = (
                roll_rows(wide[:, lanes(0)], -1) + wide[:, lanes(1)] + roll_rows(wide[:, lanes(2)], 1)
            )
            hg = total * slope[m, :, lanes(i)].astype(F32)
            hgrad[1 + i, m] = hg.astype(BF16)
            tail = jnp.zeros((lon_pad - lon, LANE), F32)
            for b in range(3):
                moved = hg if b == 1 else roll_rows(hg, b - 1)
                hgrad_t[(i * 3 + b) * LANE:(i * 3 + b + 1) * LANE, :] = jnp.transpose(
                    jnp.concatenate([moved, tail], axis=0)
                ).astype(BF16)
        send_halo(hgrad_halo, m)
        rows = jnp.concatenate([feat_rows[e, m] for e in range(4)], axis=1)
        inner_acc[...] += jnp.dot(hgrad_t[...], rows, preferred_element_type=F32)
        fields = grad_field[m].reshape(4 * VP, lon_pad)
        head_acc[...] += jnp.dot(fields, shifted[m], preferred_element_type=F32)
        return carry

    lax.fori_loop(0, members, backward, 0)

    for a in range(3):
        for b in range(3):
            ab = a * 3 + b
            ar_in[ab * LANE:(ab + 1) * LANE] = (
                inner_acc[b * LANE:(b + 1) * LANE, lanes(a)]
                + inner_acc[(3 + b) * LANE:(4 + b) * LANE, lanes(1 + a)]
            )
            base = 9 * LANE + ab * VP
            ar_in[base:base + VP] = (
                head_acc[(2 - a) * VP:(3 - a) * VP, lanes(b * 2)]
                + head_acc[(3 - a) * VP:(4 - a) * VP, lanes(b * 2 + 1)]
            )
    used = 9 * (LANE + VP)
    total_rows = ar_in.shape[0]
    ar_in[used:] = jnp.zeros((total_rows - used, LANE), F32)
    half_rows = total_rows // 2
    mem_rows = half_rows // MEM
    seat_rows = mem_rows // MEM

    def at_rows(start, size):
        return pl.ds(pl.multiple_of(start, 8), size)

    my_half = half * half_rows
    my_mem = my_half + d * mem_rows
    my_seat = my_mem + seat * seat_rows

    def rs1():
        return remote(
            ar_in.at[at_rows((1 - half) * half_rows, half_rows)], ar_r1, r1_s, r1_r, lat=partner
        )

    def rs2(k):
        return remote(
            ar_in.at[at_rows(my_half + mem_peer(k) * mem_rows, mem_rows)],
            ar_r2.at[k], r2_s.at[k], r2_r.at[k], mem=mem_peer(k),
        )

    def rs3(k):
        return remote(
            ar_in.at[at_rows(my_mem + lax.rem(seat + k, MEM) * seat_rows, seat_rows)],
            ar_r3.at[k], r3_s.at[k], r3_r.at[k], lat=lat_peer(k),
        )

    def ag3(k):
        piece = ar_out.at[at_rows(my_seat, seat_rows)]
        return remote(piece, piece, g3_s.at[k], g3_r.at[k], lat=lat_peer(k))

    def ag2(k):
        piece = ar_out.at[at_rows(my_mem, mem_rows)]
        return remote(piece, piece, g2_s.at[k], g2_r.at[k], mem=mem_peer(k))

    def ag1():
        piece = ar_out.at[at_rows(my_half, half_rows)]
        return remote(piece, piece, g1_s, g1_r, lat=partner)

    def stage_one():
        rs1().wait()
        mine = at_rows(my_half, half_rows)
        ar_in[mine] = ar_in[mine] + ar_r1[...]
        for k in range(1, MEM):
            rs2(k).start()

    def stage_two():
        for k in range(1, MEM):
            rs2(k).wait()
        mine = at_rows(my_mem, mem_rows)
        total = ar_in[mine]
        for k in range(1, MEM):
            total = total + ar_r2[k]
        ar_in[mine] = total
        for k in range(1, MEM):
            rs3(k).start()

    def stage_three():
        for k in range(1, MEM):
            rs3(k).wait()
        mine = at_rows(my_seat, seat_rows)
        total = ar_in[mine]
        for k in range(1, MEM):
            total = total + ar_r3[k]
        ar_out[mine] = total
        for k in range(1, MEM):
            ag3(k).start()

    def gf_copy(m):
        return pltpu.make_async_copy(gf_buf.at[lax.rem(m, 2)], gf_out.at[m], out_sem.at[lax.rem(m, 2)])

    rs1().start()

    def last(m, carry):
        recv_halo(hgrad_halo, m)

        @pl.when(m >= 2)
        def _():
            gf_copy(m - 2).wait()

        rows = jnp.concatenate([hgrad[e, m] for e in range(4)], axis=1)
        wide[...] = jnp.dot(rows, w_inner_back[...], preferred_element_type=F32)
        for o in range(2):
            total = (
                roll_rows(wide[:, lanes(o * 3)], -1)
                + wide[:, lanes(o * 3 + 1)]
                + roll_rows(wide[:, lanes(o * 3 + 2)], 1)
            )
            gf_buf[lax.rem(m, 2), o] = total.astype(BF16)
        gf_copy(m).start()

        @pl.when(m == 0)
        def _():
            stage_one()

        @pl.when(m == 1)
        def _():
            stage_two()

        @pl.when(m == 2)
        def _():
            stage_three()

        return carry

    lax.fori_loop(0, members, last, 0)

    for k in range(1, MEM):
        ag3(k).wait()
    for k in range(1, MEM):
        ag2(k).start()
    for m in range(members):
        drain_halo(gfield_halo, m)
        drain_halo(hgrad_halo, m)
    for k in range(1, MEM):
        ag2(k).wait()
    ag1().start()
    for m in range(max(members - 2, 0), members):
        gf_copy(m).wait()
    ag1().wait()

    points = 1.0 / (2 * LAT * lon)
    variables = gh_out.shape[2]
    for ab in range(9):
        gi_out[ab] = jnp.transpose(ar_out[ab * LANE:(ab + 1) * LANE]) * points
        base = 9 * LANE + ab * VP
        piece = jnp.concatenate(
            [ar_out[base:base + VP], jnp.zeros((LANE - VP, LANE), F32)], axis=0
        )
        gh_out[ab] = (jnp.transpose(piece) * points)[:, 0:variables]


def shards(features, conv_inner, conv_head, truth, kernel_width, var_weight):
    members, band, lon, channels = features.shape
    variables = conv_head.shape[3]
    lon_pad = -(-lon // (4 * LANE)) * 4 * LANE
    third = lon_pad // 4
    kin = conv_inner.reshape(9, channels, channels)
    ht = jnp.pad(
        jnp.swapaxes(conv_head.reshape(9, channels, variables), 1, 2),
        ((0, 0), (0, VP - variables), (0, 0)),
    )
    inverse = 1.0 / (kernel_width * kernel_width)
    scale = jnp.sqrt(0.5 * math.log2(math.e) * inverse)
    weight = var_weight * inverse / scale
    total_members = members * lax.axis_size("mem")
    prm = jnp.stack([scale, weight * (2.0 / (total_members - 1)), weight * 2.0])
    prm = jnp.broadcast_to(
        jnp.pad(prm, ((0, 0), (0, VP - variables)))[:, :, None], (3, VP, LANE)
    )
    d = lax.axis_index("mem")
    padded = jnp.pad(truth, ((0, VP - variables), (0, 0), (0, lon_pad - lon)))
    piece = lax.dynamic_slice(
        padded, (0, d // 4, lax.rem(d, 4) * third), (VP, 1, third)
    ).reshape(VP, third)

    any_spec = pl.BlockSpec(memory_space=pl.ANY)
    vmem = pl.BlockSpec(memory_space=pltpu.VMEM)
    dma = pltpu.SemaphoreType.DMA
    total_rows = 2048
    scratch = [
        pltpu.VMEM((4, members, lon_pad, LANE), BF16),
        pltpu.VMEM((lon, 6 * LANE), F32),
        pltpu.VMEM((members, lon_pad, 6 * LANE), BF16),
        pltpu.VMEM((members, lon, 2 * LANE), BF16),
        pltpu.VMEM((4, members, lon, LANE), BF16),
        pltpu.VMEM((6 * LANE, lon_pad), BF16),
        pltpu.VMEM((2, 2, VP, lon_pad), F32),
        pltpu.VMEM((MEM, members, VP, third), BF16),
        pltpu.VMEM((MEM, members, VP, third), BF16),
        pltpu.VMEM((MEM, members, VP, third), BF16),
        pltpu.VMEM((MEM, members, VP, third), BF16),
        pltpu.VMEM((members, 4, VP, lon_pad), BF16),
        pltpu.VMEM((4 * LANE, 6 * LANE), BF16),
        pltpu.VMEM((4 * VP, 6 * LANE), BF16),
        pltpu.VMEM((2 * LANE, 3 * LANE), BF16),
        pltpu.VMEM((4 * LANE, 6 * LANE), BF16),
        pltpu.VMEM((6 * LANE, 4 * LANE), F32),
        pltpu.VMEM((4 * VP, 6 * LANE), F32),
        pltpu.VMEM((total_rows, LANE), F32),
        pltpu.VMEM((total_rows, LANE), F32),
        pltpu.VMEM((total_rows // 2, LANE), F32),
        pltpu.VMEM((MEM, total_rows // 2 // MEM, LANE), F32),
        pltpu.VMEM((MEM, total_rows // 2 // MEM // MEM, LANE), F32),
        pltpu.VMEM((2, 2, lon, LANE), BF16),
        dma((members, 2)),
        dma((2, members)), dma((2, members)),
        dma((2, members)), dma((2, members)),
        dma((members, MEM)), dma((members, MEM)),
        dma((third // LANE, MEM)), dma((third // LANE, MEM)),
        dma((2, members)), dma((2, members)),
        dma((2, members)), dma((2, members)),
        dma, dma,
        dma((MEM,)), dma((MEM,)),
        dma((MEM,)), dma((MEM,)),
        dma((MEM,)), dma((MEM,)),
        dma((MEM,)), dma((MEM,)),
        dma, dma,
        dma((2,)),
    ]
    grad_features, inner, head = pl.pallas_call(
        whole_block,
        out_shape=(
            jax.ShapeDtypeStruct(features.shape, BF16),
            jax.ShapeDtypeStruct((9, channels, channels), F32),
            jax.ShapeDtypeStruct((9, channels, variables), F32),
        ),
        in_specs=[any_spec, vmem, vmem, vmem, vmem],
        out_specs=(any_spec, vmem, vmem),
        scratch_shapes=scratch,
        compiler_params=pltpu.CompilerParams(
            collective_id=0, has_side_effects=True, vmem_limit_bytes=67043328
        ),
    )(features, kin, ht, prm, piece)
    return (
        grad_features,
        inner.reshape(3, 3, channels, channels),
        head.reshape(3, 3, channels, variables),
    )


def solution(mesh):
    in_specs = (P("mem", "lat", None, None), P(), P(), P(None, "lat", None), P(), P())
    out_specs = (P("mem", "lat", None, None), P(), P())
    return jax.shard_map(shards, mesh=mesh, in_specs=in_specs, out_specs=out_specs, check_vma=False)
```

time: 698 us -> 155 us (0.22); the launches traced: 687 us -> 155 us
  matrix products: 210 us -> 0 us
  waiting for transfers between devices: 204 us -> 0 us
  Pallas kernels: 0 us -> 142 us
  local copies, waits for them, and re-layouts: 98.7 us -> 10.9 us
  other arithmetic: 81.2 us -> 1.35 us
  starting transfers between devices: 54.5 us -> 0 us
  blocking collectives: 22.8 us -> 0 us
  between operations: 15 us -> 0.68 us
    dot_general x54 -> x0, matrix products: 210 us -> none  [the longest x9 53.3 us: field_back(): jnp.einsum('mvrl,cv->mrlc', padded_grad[:, :, 2 - row_off:2 - row_off + b...]
    psum x1 -> x0, waiting for transfers between devices: 145 us -> none  [shards(): inner_sum, head_sum = lax.psum((inner_grad, head_grad), ('mem', 'lat'))]
    pallas_call x0 -> x1, Pallas kernels: none -> 142 us  [shards(): pl.pallas_call(whole_block, out_shape=(jax.ShapeDtypeStruct(features.shap...]
    reduce_sum x23 -> x0, other arithmetic: 52.8 us -> none  [pair_sums(): return jnp.sum(kernel * spread, axis=1)]
    ppermute x8 -> x0, starting transfers between devices: 47 us -> none  [the longest x4 38.9 us: padded_2(): lax.ppermute(tail, axis, [(i, (i + 1) % count) for i in range(ends)])]
    ppermute x8 -> x0, waiting for transfers between devices: 35.5 us -> none  [the longest x4 25 us: padded_2(): lax.ppermute(tail, axis, [(i, (i + 1) % count) for i in range(ends)])]
    all_to_all x1 -> x0, waiting for transfers between devices: 23.6 us -> none  [shards(): lax.all_to_all(field, 'mem', split_axis=3, concat_axis=0, tiled=True)]
    all_to_all x1 -> x0, blocking collectives: 22.8 us -> none  [shards(): lax.all_to_all(gradient, 'mem', split_axis=0, concat_axis=3, tiled=True)]
  transfers between devices with their start and end apart: 10 -> 0, of which waited for: 8 -> 0; matrix products, arithmetic and copies ran while one was open for 4% -> 0% of each run, Pallas kernels for 0% -> 0%
where the time goes in v1:
time: 155 us
  Pallas kernels  142 us (92%)
  local copies, waits for them, and re-layouts  10.9 us (7%)
    pallas_call x1, Pallas kernels, shards(): pl.pallas_call(whole_block, out_shape=(jax.ShapeDtypeStruct(features.shap...  142 us
    unnamed x6, local copies, waits for them, and re-layouts  7.85 us

profile of v1, /device:TPU:1, one launch (start us, length us, event | category | flops | bytes accessed | tf_op | source)
XLA Modules:
  0.0 154.8 jit_solution(15555325895297942217)
XLA Ops:
  0.7 0.7 fusion.1
  1.3 0.7 multiply_bitcast_fusion.1
  2.0 0.8 broadcast_in_dim.2.prm
  2.8 1.6 %pad.12.ht = bf16[9,80,128]{2,1,0:T(8,128)(2,1)} pad(bf16[9,69,128]{2,1,0:T(8,128)(2,1)} %bitcast.17, bf16[]{:T(256)} %constant.12.clone.1), padding=0_0x0_11x0_0 | pad | bytes 343298 | tf_op jit(solution)/shard_map/jit(_pad)/pad | solution.py:524
  4.4 1.3 copy.10
  5.7 0.7 fusion.truth
  6.4 141.9 %shard_map.85 = (bf16[4,2,1440,128]{3,2,1,0:T(8,128)(2,1)}, f32[9,128,128]{2,1,0:T(8,128)}, f32[9,128,69]{2,1,0:T(8,128)}) custom-call(bf16[4,2,1440,128]{3,2,1,0:T(8,128)(2,1)} %feat.1, bf16[9,128,128]{2,1,0:T(8,128)(2,1)} %bitcast.16, bf16[9,80,128]{2,1,0:T(8,128)(2,1)} %pad.12.ht, f32[3,80,128]{2,1,0:T(8,128)} %broadcast_in_dim.2.prm, f32[80,384]{1,0:T(8,128)} %fusion.truth), custom_call_target="tpu_custom_call" | custom-call | tf_op jit(solution)/shard_map/pallas_call | solution.py:586
  148.3 2.0 %copy.11 = f32[3,3,128,69]{2,3,1,0:T(8,128)} copy(f32[3,3,128,69]{3,2,1,0:T(8,128)} %bitcast.14) | data formatting | bytes 635904
  150.3 0.0 copy-start
  150.3 3.7 %copy.14 = bf16[4,2,1440,128]{3,2,1,0:T(8,128)(2,1)} copy(bf16[4,2,1440,128]{3,2,1,0:T(8,128)(2,1)} %get-tuple-element.22) | data formatting | bytes 5898240
  154.0 0.0 copy-done
  154.0 0.8 copy.15
  (2 shorter events, 0.0 us)
Async XLA Ops:
  150.3 3.7 %copy-start = (f32[9,128,128]{2,1,0:T(8,128)S(1)}, f32[9,128,128]{2,1,0:T(8,128)}, u32[]{:S(2)}) copy-start(f32[9,128,128]{2,1,0:T(8,128)} %get-tuple-element.7) | copy-start | bytes 1769476

commit v2 on v1

v2 whole, which is shorter than its diff:
```python
import math
import jax
import jax.numpy as jnp
from jax import lax
from jax.experimental import pallas as pl
from jax.experimental.pallas import tpu as pltpu
from jax.sharding import PartitionSpec as P

MESH_ID = pl.DeviceIdType.MESH
F32 = jnp.float32
BF16 = jnp.bfloat16
LANE = 128
VP = 80
MEM = 8
LAT = 16
HEAD_ROWS = 768
RELAYS = (0, LAT - 1)
GELU_A = math.sqrt(2.0 / math.pi)
GELU_B = 0.044715


def roll_rows(values, shift):
    return pltpu.roll(values, shift % values.shape[0], 0)


def transposed(values):
    return jnp.transpose(values.astype(F32)).astype(BF16)


def whole_block(
    feat, kin, ht, width, weight, truth,
    gf_out, gi_out, gh_out,
    feat_rows, wide, shifted, slope, hgrad, hgrad_t, own_field,
    part_out, part_in, field_out, values_in, grad_field,
    w_inner, w_head, w_head_back, w_inner_back,
    feat_relay, part_relay, gfield_relay, hgrad_relay,
    inner_acc, head_acc, gf_buf, prm, target_buf,
    hs_in, hs_out, hs_r1, hs_r2, hs_r3, is_in, is_out, is_r1, is_r2, is_r3,
    load_sem, fh_s, fh_r, ph_s, ph_r, a2_s, a2_r, b2_s, b2_r, gh_s, gh_r, hh_s, hh_r,
    hsum_sems, isum_sems, out_sem, relay_s, relay_r,
):
    lon = feat.shape[2]
    lon_pad = grad_field.shape[3]
    members = feat.shape[0]
    third = lon_pad // 4
    d = lax.axis_index("mem")
    r = lax.axis_index("lat")
    has_up = r > 0
    has_down = r < LAT - 1
    above = lax.rem(r + LAT - 1, LAT)
    below = lax.rem(r + 1, LAT)
    half = lax.rem(r, 2)
    seat = r // 2

    def mem_peer(k):
        return lax.rem(d + k, MEM)

    def lat_peer(k):
        return lax.rem(seat + k, MEM) * 2 + half

    partner = r + 1 - 2 * half

    def remote(src, dst, ss, rs, **where):
        return pltpu.make_async_remote_copy(
            src_ref=src, dst_ref=dst, send_sem=ss, recv_sem=rs,
            device_id=where, device_id_type=MESH_ID,
        )

    barrier = pltpu.get_barrier_semaphore()
    for k in range(1, MEM):
        pl.semaphore_signal(barrier, inc=1, device_id={"mem": mem_peer(k)}, device_id_type=MESH_ID)
    for k in range(1, LAT):
        pl.semaphore_signal(
            barrier, inc=1, device_id={"lat": lax.rem(r + k, LAT)}, device_id_type=MESH_ID
        )

    def load(m, row):
        return pltpu.make_async_copy(
            feat.at[m, row], feat_rows.at[1 + row, m, pl.ds(0, lon)], load_sem.at[m, row]
        )

    for m in range(members):
        for row in range(2):
            load(m, row).start()

    pl.semaphore_wait(barrier, MEM - 1 + LAT - 1)

    mid_up = r == LAT // 2 - 1
    mid_down = r == LAT // 2
    relay_down = RELAYS[0]
    relay_up = RELAYS[1]
    is_relay = jnp.logical_or(r == relay_down, r == relay_up)
    relay_end = jnp.where(r == relay_down, LAT // 2, LAT // 2 - 1)
    part_rows = lon // 2

    def halo_rows(part):
        return pl.ds(part * part_rows, part_rows)

    def feat_ends(side, part, m):
        own, other = (1, 3) if side == 0 else (2, 0)
        return feat_rows.at[own, m, halo_rows(part)], feat_rows.at[other, m, halo_rows(part)]

    def part_ends(side, part, m):
        slots = pl.ds(side * 4 + part * 2, 2)
        return part_out.at[slots, m], part_in.at[slots, m]

    def gfield_ends(side, part, t):
        own, other = (1, 3) if side == 0 else (2, 0)
        rows = pl.ds(pl.multiple_of(t * 16, 16), 16)
        half_members = pl.ds(part * (members // 2), members // 2)
        return grad_field.at[half_members, own, rows], grad_field.at[half_members, other, rows]

    def hgrad_ends(side, part, m):
        own, other = (1, 3) if side == 0 else (2, 0)
        return hgrad.at[own, m, halo_rows(part)], hgrad.at[other, m, halo_rows(part)]

    feat_halo = (feat_ends, fh_s, fh_r, feat_relay, 0)
    part_halo = (part_ends, ph_s, ph_r, part_relay, 1)
    gfield_halo = (gfield_ends, gh_s, gh_r, gfield_relay, 2)
    hgrad_halo = (hgrad_ends, hh_s, hh_r, hgrad_relay, 3)

    sides = (
        (0, has_up, has_down, above, mid_down, relay_up),
        (1, has_down, has_up, below, mid_up, relay_down),
    )

    def direct(kind, side, part, m, where):
        ends, ss, rs, _, _ = kind
        src, dst = ends(side, part, m)
        return remote(src, dst, ss.at[side * 2 + part, m], rs.at[side * 2 + part, m], lat=where)

    def to_relay(kind, side, m, where):
        ends, ss, _, buffer, row = kind
        return remote(ends(side, 1, m)[0], buffer.at[m], ss.at[side * 2 + 1, m], relay_r.at[row, m], lat=where)

    def from_relay(kind, side, m):
        ends, _, rs, buffer, row = kind
        return remote(
            buffer.at[m], ends(side, 1, m)[1], relay_s.at[row, m], rs.at[side * 2 + 1, m], lat=relay_end
        )

    def send_halo(kind, m):
        for side, sends, _, where, by_relay, relay in sides:
            @pl.when(jnp.logical_and(sends, jnp.logical_not(by_relay)))
            def _():
                direct(kind, side, 0, m, where).start()
                direct(kind, side, 1, m, where).start()

            @pl.when(by_relay)
            def _():
                to_relay(kind, side, m, relay).start()
                direct(kind, side, 0, m, where).start()

    def recv_halo(kind, m):
        for side, _, receives, where, _, _ in sides:
            @pl.when(receives)
            def _():
                direct(kind, side, 0, m, where).wait_recv()
                direct(kind, side, 1, m, where).wait_recv()

    def drain_halo(kind, m):
        for side, sends, _, where, _, _ in sides:
            @pl.when(sends)
            def _():
                direct(kind, side, 0, m, where).wait_send()
                direct(kind, side, 1, m, where).wait_send()

        for side, relay in ((0, relay_up), (1, relay_down)):
            @pl.when(r == relay)
            def _():
                from_relay(kind, side, m).wait_send()

    def pass_on(kind, m):
        for side, relay in ((0, relay_up), (1, relay_down)):
            @pl.when(r == relay)
            def _():
                to_relay(kind, side, m, relay_end).wait_recv()
                from_relay(kind, side, m).start()

    for m in range(members):
        for row in range(2):
            load(m, row).wait()
        send_halo(feat_halo, m)

    feat_rows[:, :, lon:, :] = jnp.zeros((4, members, lon_pad - lon, LANE), BF16)
    shifted[:, lon:, :] = jnp.zeros((members, lon_pad - lon, shifted.shape[2]), BF16)

    @pl.when(r == 0)
    def _():
        for m in range(members):
            feat_rows[0, m, 0:lon] = jnp.zeros((lon, LANE), BF16)
            hgrad[0, m] = jnp.zeros((lon, LANE), BF16)
            grad_field[m, 0] = jnp.zeros((VP, lon_pad), BF16)
            for q in range(4):
                part_in[4 + q, m] = jnp.zeros((VP, third), BF16)

    @pl.when(r == LAT - 1)
    def _():
        for m in range(members):
            feat_rows[3, m, 0:lon] = jnp.zeros((lon, LANE), BF16)
            hgrad[3, m] = jnp.zeros((lon, LANE), BF16)
            grad_field[m, 3] = jnp.zeros((VP, lon_pad), BF16)
            for q in range(4):
                part_in[q, m] = jnp.zeros((VP, third), BF16)

    w_inner[...] = jnp.zeros(w_inner.shape, BF16)
    w_inner_back[...] = jnp.zeros(w_inner_back.shape, BF16)
    w_head[...] = jnp.zeros(w_head.shape, BF16)
    w_head_back[...] = jnp.zeros(w_head_back.shape, BF16)
    for a in range(3):
        for b in range(3):
            block = kin[a * 3 + b]
            block_t = transposed(block)
            head_t = ht[a * 3 + b]
            nv = head_t.shape[0]
            for o in range(2):
                cols = slice((o * 3 + b) * LANE, (o * 3 + b + 1) * LANE)
                w_inner[(o + a) * LANE:(o + a + 1) * LANE, cols] = block
                e = o - a + 2
                w_inner_back[e * LANE:(e + 1) * LANE, cols] = block_t
                row = o - a + 2
                w_head[row * VP:row * VP + nv, b * 2 * LANE + o * LANE:b * 2 * LANE + (o + 1) * LANE] = head_t
            w_head_back[(2 - a) * VP:(2 - a) * VP + nv, b * LANE:(b + 1) * LANE] = head_t

    def column(ref, fill):
        nv = ref.shape[1]
        row = jnp.concatenate([ref[...], jnp.full((1, LANE - nv), fill, F32)], axis=1)
        return jnp.transpose(jnp.broadcast_to(row, (LANE, LANE)))[0:VP]

    widths = column(width, 1.0)
    inverse = 1.0 / (widths * widths)
    scaling = jnp.sqrt(0.5 * math.log2(math.e) * inverse)
    factor = column(weight, 0.0) * inverse / scaling
    prm[0] = scaling
    prm[1] = factor * (2.0 / (MEM * members - 1))
    prm[2] = factor * 2.0
    target_buf[...] = jnp.zeros(target_buf.shape, F32)
    for quarter in range(4):
        for row in range(2):
            @pl.when(d == row * 4 + quarter)
            def _():
                stop = min((quarter + 1) * third, lon)
                target_buf[0:truth.shape[0], 0:stop - quarter * third] = truth[:, row, quarter * third:stop]

    def lanes(index):
        return slice(index * LANE, (index + 1) * LANE)

    def forward(m):
        recv_halo(feat_halo, m)
        rows = jnp.concatenate([feat_rows[e, m, 0:lon] for e in range(4)], axis=1)
        wide[...] = jnp.dot(rows, w_inner[...], preferred_element_type=F32)
        for o in range(2):
            pre = (
                roll_rows(wide[:, lanes(o * 3)], 1)
                + wide[:, lanes(o * 3 + 1)]
                + roll_rows(wide[:, lanes(o * 3 + 2)], -1)
            )
            square = pre * pre
            th = jnp.tanh(GELU_A * pre * (1.0 + GELU_B * square))
            cdf = 0.5 + 0.5 * th
            hidden = pre * cdf
            grad = cdf + 0.5 * pre * (1.0 - th * th) * (GELU_A * (1.0 + 3.0 * GELU_B * square))
            slope[m, :, lanes(o)] = grad.astype(BF16)
            shifted[m, 0:lon, lanes(o)] = roll_rows(hidden, 1).astype(BF16)
            shifted[m, 0:lon, lanes(2 + o)] = hidden.astype(BF16)
            shifted[m, 0:lon, lanes(4 + o)] = roll_rows(hidden, -1).astype(BF16)
        slot = m
        for q in range(4):
            sums = lax.dot_general(
                w_head[...], shifted[m, q * third:(q + 1) * third, :],
                (((1,), (1,)), ((), ())), preferred_element_type=F32,
            )
            part_out[q, m] = sums[0:VP].astype(BF16)
            own_field[slot, 0, :, q * third:(q + 1) * third] = sums[VP:2 * VP]
            own_field[slot, 1, :, q * third:(q + 1) * third] = sums[2 * VP:3 * VP]
            part_out[4 + q, m] = sums[3 * VP:4 * VP].astype(BF16)
        send_halo(part_halo, m)

    chunks = VP // 16

    def tile(t):
        return pl.ds(t * 16 if isinstance(t, int) else pl.multiple_of(t * 16, 16), 16)

    def field_copy(m, t, k):
        p = mem_peer(k)
        return remote(
            field_out.at[p, m, tile(t)], values_in.at[d, m, tile(t)],
            a2_s.at[m * chunks + t, k], a2_r.at[m * chunks + t, k], mem=p,
        )

    def finish_field(m):
        recv_halo(part_halo, m)
        slot = m
        for row in range(2):
            for q in range(4):
                total = own_field[slot, row, :, q * third:(q + 1) * third] + part_in[
                    (1 - row) * 4 + q, m
                ].astype(F32)
                field_out[row * 4 + q, m] = total.astype(BF16)
        for t in range(chunks):
            for k in range(1, MEM):
                field_copy(m, t, k).start()
        values_in[d, m] = field_out[d, m]

    for m in range(members):
        pass_on(feat_halo, m)

    def forward_step(m, carry):
        forward(m)

        @pl.when(m > 0)
        def _():
            pass_on(part_halo, m - 1)

        return carry

    def finish_step(m, carry):
        finish_field(m)
        return carry

    lax.fori_loop(0, members, forward_step, 0)
    pass_on(part_halo, members - 1)
    lax.fori_loop(0, members, finish_step, 0)

    grad_out = field_out
    count = MEM * members
    own_row = 1 + d // 4
    own_lane = lax.rem(d, 4) * third

    def place(j):
        return slice((j // 2) * 16, (j // 2 + 1) * 16), slice((j % 2) * third, (j % 2 + 1) * third)

    def back_copy(t, k):
        p = mem_peer(k)
        rows = tile(t)
        return remote(
            grad_out.at[p, :, rows],
            grad_field.at[:, own_row, rows, pl.ds(pl.multiple_of(own_lane, LANE), third)],
            b2_s.at[t, k], b2_r.at[t, k], mem=p,
        )

    block = 8
    lane_groups = third // LANE
    used_groups = -(-truth.shape[0] // 8)

    def pair_chunk(t, carry):
        rows16 = tile(t)

        def arrived(m, inner):
            for k in range(1, MEM):
                field_copy(m, t, k).wait()
            return inner

        lax.fori_loop(0, members, arrived, 0)
        scale = jnp.concatenate([prm[0, rows16]] * lane_groups, axis=1)
        for j in range(count):
            rows, cols = place(j)
            wide[rows, cols] = values_in[j // members, j % members, rows16].astype(F32) * scale

        def group(unit, inner):
            sub = unit // lane_groups
            lane = lax.rem(unit, lane_groups) * LANE

            def at(j):
                return (
                    pl.ds(pl.multiple_of((j // 2) * 16 + sub * 8, 8), 8),
                    pl.ds(pl.multiple_of((j % 2) * third + lane, LANE), LANE),
                )

            rows8 = pl.ds(pl.multiple_of(t * 16 + sub * 8, 8), 8)
            target = target_buf[rows8, pl.ds(pl.multiple_of(lane, LANE), LANE)] * prm[0, rows8]
            pair_weight = prm[1, rows8]
            truth_weight = prm[2, rows8]

            def term(x, y):
                u = x - y
                return u * jnp.exp2(u * (y - x))

            for i0 in range(0, count, block):
                xi = [wide[at(i0 + i)] for i in range(block)]
                sums = [None] * block
                for i in range(block):
                    for j in range(i + 1, block):
                        w = term(xi[j], xi[i])
                        sums[i] = w if sums[i] is None else sums[i] + w
                        sums[j] = -w if sums[j] is None else sums[j] - w
                if i0 > 0:
                    sums = [s + wide[at(count + i0 + i)] for i, s in enumerate(sums)]
                for j0 in range(i0 + block, count, 4):
                    xj = [wide[at(j0 + j)] for j in range(4)]
                    back = [None] * 4
                    for j in range(4):
                        for i in range(block):
                            w = term(xj[j], xi[i])
                            sums[i] = sums[i] + w
                            back[j] = -w if back[j] is None else back[j] - w
                    for j in range(4):
                        old = back[j] if i0 == 0 else wide[at(count + j0 + j)] + back[j]
                        wide[at(count + j0 + j)] = old
                for i in range(block):
                    near = term(xi[i], target)
                    wide[at(count + i0 + i)] = pair_weight * sums[i] + truth_weight * near
            return inner

        subs = jnp.minimum(2, used_groups - 2 * t)
        lax.fori_loop(0, subs * lane_groups, group, 0)
        keep = lax.broadcasted_iota(jnp.int32, (16, third), 0) < subs * 8
        for j in range(count):
            rows, cols = place(count + j)
            grad_out[j // members, j % members, rows16] = jnp.where(keep, wide[rows, cols], 0.0).astype(BF16)
        for k in range(1, MEM):
            back_copy(t, k).start()
        grad_field[:, own_row, rows16, pl.ds(pl.multiple_of(own_lane, LANE), third)] = grad_out[d, :, rows16]
        return carry

    lax.fori_loop(0, chunks, pair_chunk, 0)

    def wait_back(t, carry):
        for k in range(1, MEM):
            back_copy(t, k).wait()
        send_halo(gfield_halo, t)
        return carry

    lax.fori_loop(0, chunks, wait_back, 0)

    inner_acc[...] = jnp.zeros(inner_acc.shape, F32)
    head_acc[...] = jnp.zeros(head_acc.shape, F32)

    def at_rows(start, size):
        return pl.ds(pl.multiple_of(start, 8), size)

    def device_sum(src, dst, r1, r2, r3, sems):
        half_rows = src.shape[0] // 2
        piece_rows = half_rows // MEM
        my_half = half * half_rows
        my_piece = my_half + d * piece_rows
        s1, s2, s3, s4, s5 = [(sems.at[2 * n], sems.at[2 * n + 1]) for n in range(5)]

        def scatter_pair():
            return remote(
                src.at[at_rows((1 - half) * half_rows, half_rows)], r1, s1[0].at[0], s1[1].at[0], lat=partner
            )

        def scatter(k):
            return remote(
                src.at[at_rows(my_half + mem_peer(k) * piece_rows, piece_rows)],
                r2.at[k], s2[0].at[k], s2[1].at[k], mem=mem_peer(k),
            )

        def share(k):
            return remote(src.at[at_rows(my_piece, piece_rows)], r3.at[seat], s3[0].at[k], s3[1].at[k], lat=lat_peer(k))

        def gather(k):
            piece = dst.at[at_rows(my_piece, piece_rows)]
            return remote(piece, piece, s4[0].at[k], s4[1].at[k], mem=mem_peer(k))

        def gather_pair():
            piece = dst.at[at_rows(my_half, half_rows)]
            return remote(piece, piece, s5[0].at[0], s5[1].at[0], lat=partner)

        def each(copy_of, act):
            for k in range(1, MEM):
                act(copy_of(k))

        start = lambda c: c.start()
        wait = lambda c: c.wait()

        def step_0():
            scatter_pair().start()

        def step_1():
            scatter_pair().wait()
            mine = at_rows(my_half, half_rows)
            src[mine] = src[mine] + r1[...]
            each(scatter, start)

        def step_2():
            each(scatter, wait)
            mine = at_rows(my_piece, piece_rows)
            total = src[mine]
            for k in range(1, MEM):
                total = total + r2[k]
            src[mine] = total
            each(share, start)
            r3[seat] = total

        def step_3():
            each(share, wait)
            total = r3[0]
            for k in range(1, MEM):
                total = total + r3[k]
            dst[at_rows(my_piece, piece_rows)] = total * (1.0 / (2 * LAT * lon))
            each(gather, start)

        def step_4():
            each(gather, wait)
            gather_pair().start()

        def step_5():
            gather_pair().wait()

        return step_0, step_1, step_2, step_3, step_4, step_5

    head_steps = device_sum(hs_in, hs_out, hs_r1, hs_r2, hs_r3, hsum_sems)
    inner_steps = device_sum(is_in, is_out, is_r1, is_r2, is_r3, isum_sems)

    def head_gradient(m, carry):
        fields = grad_field[m].reshape(4 * VP, lon_pad)
        head_acc[...] += jnp.dot(fields, shifted[m], preferred_element_type=F32)
        return carry

    def halo_tiles(t, carry):
        pass_on(gfield_halo, t)
        recv_halo(gfield_halo, t)
        return carry

    lax.fori_loop(0, chunks, halo_tiles, 0)
    lax.fori_loop(0, members, head_gradient, 0)
    for a in range(3):
        for b in range(3):
            base = (a * 3 + b) * VP
            hs_in[base:base + VP] = (
                head_acc[(2 - a) * VP:(3 - a) * VP, lanes(b * 2)]
                + head_acc[(3 - a) * VP:(4 - a) * VP, lanes(b * 2 + 1)]
            )
    hs_in[9 * VP:] = jnp.zeros((hs_in.shape[0] - 9 * VP, LANE), F32)
    head_steps[0]()

    def backward(m, carry):
        for i in range(2):
            stack = [grad_field[m, i + j] for j in range(3)]
            stack.append(jnp.zeros((2 * LANE - 3 * VP, lon_pad), BF16))
            columns = transposed(jnp.concatenate(stack, axis=0))
            wide[:, 0:3 * LANE] = jnp.dot(
                columns[0:lon], w_head_back[...], preferred_element_type=F32
            )
            total = (
                roll_rows(wide[:, lanes(0)], -1) + wide[:, lanes(1)] + roll_rows(wide[:, lanes(2)], 1)
            )
            hg = total * slope[m, :, lanes(i)].astype(F32)
            hgrad[1 + i, m] = hg.astype(BF16)
            tail = jnp.zeros((lon_pad - lon, LANE), F32)
            for b in range(3):
                moved = hg if b == 1 else roll_rows(hg, b - 1)
                hgrad_t[(i * 3 + b) * LANE:(i * 3 + b + 1) * LANE, :] = jnp.transpose(
                    jnp.concatenate([moved, tail], axis=0)
                ).astype(BF16)
        send_halo(hgrad_halo, m)
        rows = jnp.concatenate([feat_rows[e, m] for e in range(4)], axis=1)
        inner_acc[...] += jnp.dot(hgrad_t[...], rows, preferred_element_type=F32)
        @pl.when(m >= 1)
        def _():
            pass_on(hgrad_halo, m - 1)

        @pl.when(m == 1)
        def _():
            head_steps[1]()

        return carry

    lax.fori_loop(0, members, backward, 0)
    for a in range(3):
        for b in range(3):
            ab = a * 3 + b
            is_in[ab * LANE:(ab + 1) * LANE] = jnp.transpose(
                inner_acc[b * LANE:(b + 1) * LANE, lanes(a)]
                + inner_acc[(3 + b) * LANE:(4 + b) * LANE, lanes(1 + a)]
            )

    def gf_copy(m):
        return pltpu.make_async_copy(gf_buf.at[lax.rem(m, 2)], gf_out.at[m], out_sem.at[lax.rem(m, 2)])

    inner_steps[0]()
    pass_on(hgrad_halo, members - 1)

    def last(m, carry):
        recv_halo(hgrad_halo, m)

        @pl.when(m >= 2)
        def _():
            gf_copy(m - 2).wait()

        rows = jnp.concatenate([hgrad[e, m] for e in range(4)], axis=1)
        wide[...] = jnp.dot(rows, w_inner_back[...], preferred_element_type=F32)
        for o in range(2):
            total = (
                roll_rows(wide[:, lanes(o * 3)], -1)
                + wide[:, lanes(o * 3 + 1)]
                + roll_rows(wide[:, lanes(o * 3 + 2)], 1)
            )
            gf_buf[lax.rem(m, 2), o] = total.astype(BF16)
        gf_copy(m).start()

        for n in range(members):
            @pl.when(m == n)
            def _():
                if n > 0:
                    head_steps[n + 1]()
                inner_steps[n + 1]()

        return carry

    lax.fori_loop(0, members, last, 0)

    for m in range(members):
        drain_halo(feat_halo, m)
        drain_halo(part_halo, m)
        drain_halo(hgrad_halo, m)
    for t in range(chunks):
        drain_halo(gfield_halo, t)
    for m in range(max(members - 2, 0), members):
        gf_copy(m).wait()
    head_steps[5]()
    for ab in range(9):
        gh_out[ab] = hs_out[ab * VP:ab * VP + gh_out.shape[1]]
    inner_steps[5]()
    for ab in range(9):
        gi_out[ab] = is_out[ab * LANE:(ab + 1) * LANE]


def sum_scratch(rows):
    piece = rows // 2 // MEM
    return [
        pltpu.VMEM((rows, LANE), F32),
        pltpu.VMEM((rows, LANE), F32),
        pltpu.VMEM((rows // 2, LANE), F32),
        pltpu.VMEM((MEM, piece, LANE), F32),
        pltpu.VMEM((MEM, piece, LANE), F32),
    ]


def shards(features, conv_inner, conv_head, truth, kernel_width, var_weight):
    members, band, lon, channels = features.shape
    variables = conv_head.shape[3]
    lon_pad = -(-lon // (4 * LANE)) * 4 * LANE
    third = lon_pad // 4
    kin = conv_inner.reshape(9, channels, channels)
    ht = jnp.swapaxes(conv_head.reshape(9, channels, variables), 1, 2)
    width = kernel_width.reshape(1, variables)
    weight = var_weight.reshape(1, variables)

    any_spec = pl.BlockSpec(memory_space=pl.ANY)
    vmem = pl.BlockSpec(memory_space=pltpu.VMEM)
    dma = pltpu.SemaphoreType.DMA
    scratch = [
        pltpu.VMEM((4, members, lon_pad, LANE), BF16),
        pltpu.VMEM((lon, 6 * LANE), F32),
        pltpu.VMEM((members, lon_pad, 6 * LANE), BF16),
        pltpu.VMEM((members, lon, 2 * LANE), BF16),
        pltpu.VMEM((4, members, lon, LANE), BF16),
        pltpu.VMEM((6 * LANE, lon_pad), BF16),
        pltpu.VMEM((members, 2, VP, lon_pad), F32),
        pltpu.VMEM((MEM, members, VP, third), BF16),
        pltpu.VMEM((MEM, members, VP, third), BF16),
        pltpu.VMEM((MEM, members, VP, third), BF16),
        pltpu.VMEM((MEM, members, VP, third), BF16),
        pltpu.VMEM((members, 4, VP, lon_pad), BF16),
        pltpu.VMEM((4 * LANE, 6 * LANE), BF16),
        pltpu.VMEM((4 * VP, 6 * LANE), BF16),
        pltpu.VMEM((2 * LANE, 3 * LANE), BF16),
        pltpu.VMEM((4 * LANE, 6 * LANE), BF16),
        pltpu.VMEM((members, lon // 2, LANE), BF16),
        pltpu.VMEM((members, 2, VP, third), BF16),
        pltpu.VMEM((VP // 16, members // 2, 16, lon_pad), BF16),
        pltpu.VMEM((members, lon // 2, LANE), BF16),
        pltpu.VMEM((6 * LANE, 4 * LANE), F32),
        pltpu.VMEM((4 * VP, 6 * LANE), F32),
        pltpu.VMEM((2, 2, lon, LANE), BF16),
        pltpu.VMEM((3, VP, LANE), F32),
        pltpu.VMEM((VP, third), F32),
        *sum_scratch(HEAD_ROWS),
        *sum_scratch(9 * LANE),
        dma((members, 2)),
        dma((4, members)), dma((4, members)),
        dma((4, members)), dma((4, members)),
        dma((members * VP // 16, MEM)), dma((members * VP // 16, MEM)),
        dma((VP // 16, MEM)), dma((VP // 16, MEM)),
        dma((4, VP // 16)), dma((4, VP // 16)),
        dma((4, members)), dma((4, members)),
        dma((10, MEM)), dma((10, MEM)),
        dma((2,)),
        dma((4, VP // 16)), dma((4, VP // 16)),
    ]
    grad_features, inner, head = pl.pallas_call(
        whole_block,
        out_shape=(
            jax.ShapeDtypeStruct(features.shape, BF16),
            jax.ShapeDtypeStruct((9, channels, channels), F32),
            jax.ShapeDtypeStruct((9, variables, channels), F32),
        ),
        in_specs=[any_spec, vmem, vmem, vmem, vmem, vmem],
        out_specs=(any_spec, vmem, vmem),
        scratch_shapes=scratch,
        compiler_params=pltpu.CompilerParams(
            collective_id=0, has_side_effects=True, vmem_limit_bytes=67043328
        ),
    )(features, kin, ht, width, weight, truth)
    return (
        grad_features,
        inner.reshape(3, 3, channels, channels),
        jnp.swapaxes(head, 1, 2).reshape(3, 3, channels, variables),
    )


def solution(mesh):
    in_specs = (P("mem", "lat", None, None), P(), P(), P(None, "lat", None), P(), P())
    out_specs = (P("mem", "lat", None, None), P(), P())
    return jax.shard_map(shards, mesh=mesh, in_specs=in_specs, out_specs=out_specs, check_vma=False)
```

time: 155 us -> 143 us (0.923)
  local copies, waits for them, and re-layouts: 10.9 us -> 5.25 us
  Pallas kernels: 142 us -> 137 us
    pallas_call x1, Pallas kernels: 142 us -> 137 us  [shards(): pl.pallas_call(whole_block, out_shape=(jax.ShapeDtypeStruct(features.shap...]
    unnamed x6 -> x7, local copies, waits for them, and re-layouts: 7.85 us -> 5.25 us
    pad x1 -> x0, local copies, waits for them, and re-layouts: 1.6 us -> none  [shards(): jnp.pad(jnp.swapaxes(conv_head.reshape(9, channels, variables), 1, 2), ((...]
where the time goes in v2:
time: 143 us
  Pallas kernels  137 us (96%)
  local copies, waits for them, and re-layouts  5.25 us (4%)
    pallas_call x1, Pallas kernels, shards(): pl.pallas_call(whole_block, out_shape=(jax.ShapeDtypeStruct(features.shap...  137 us
    unnamed x7, local copies, waits for them, and re-layouts  5.25 us

profile of v2, /device:TPU:1, one launch (start us, length us, event | category | flops | bytes accessed | tf_op | source)
XLA Modules:
  0.0 142.9 jit_solution(15156993793340090784)
XLA Ops:
  0.6 137.0 %shard_map.85 = (bf16[4,2,1440,128]{3,2,1,0:T(8,128)(2,1)}, f32[9,128,128]{2,1,0:T(8,128)}, f32[9,69,128]{2,1,0:T(8,128)}) custom-call(bf16[4,2,1440,128]{3,2,1,0:T(8,128)(2,1)} %feat.1, bf16[9,128,128]{2,1,0:T(8,128)(2,1)} %bitcast.12, bf16[9,69,128]{2,1,0:T(8,128)(2,1)} %bitcast.13, f32[1,69]{1,0:T(1,128)} %bitcast.14, f32[1,69]{1,0:T(1,128)} %bitcast.15, ...), custom_call_target="tpu_custom_call" | custom-call | tf_op jit(solution)/shard_map/pallas_call | solution.py:684
  137.7 0.0 copy-start
  137.7 0.0 copy-start.1
  137.7 3.7 %copy.12 = bf16[4,2,1440,128]{3,2,1,0:T(8,128)(2,1)} copy(bf16[4,2,1440,128]{3,2,1,0:T(8,128)(2,1)} %get-tuple-element.12) | data formatting | bytes 5898240
  141.4 0.0 copy-done
  141.4 0.8 copy.13
  142.2 0.0 copy-done.1
  142.2 0.7 copy.14
Async XLA Ops:
  137.7 3.7 %copy-start = (f32[9,128,128]{2,1,0:T(8,128)S(1)}, f32[9,128,128]{2,1,0:T(8,128)}, u32[]{:S(2)}) copy-start(f32[9,128,128]{2,1,0:T(8,128)} %get-tuple-element.7) | copy-start | bytes 1769476
  137.7 4.5 %copy-start.1 = (f32[9,69,128]{2,1,0:T(8,128)S(1)}, f32[9,69,128]{2,1,0:T(8,128)}, u32[]{:S(2)}) copy-start(f32[9,69,128]{2,1,0:T(8,128)} %get-tuple-element.8) | copy-start | bytes 953860

commit v3 on v2

--- a/solution.py
+++ b/solution.py
@@ -76,7 +76,7 @@
 
     def load(m, row):
         return pltpu.make_async_copy(
-            feat.at[m, row], feat_rows.at[1 + row, m, pl.ds(0, lon)], load_sem.at[m, row]
+            feat.at[m, row], feat_rows.at[1 + row, m, pl.ds(0, lon)], load_sem.at[m]
         )
 
     for m in range(members):
@@ -94,21 +94,21 @@
     part_rows = lon // 2
 
     def halo_rows(part):
-        return pl.ds(part * part_rows, part_rows)
+        return pl.ds(0, lon) if part is None else pl.ds(part * part_rows, part_rows)
 
     def feat_ends(side, part, m):
         own, other = (1, 3) if side == 0 else (2, 0)
         return feat_rows.at[own, m, halo_rows(part)], feat_rows.at[other, m, halo_rows(part)]
 
     def part_ends(side, part, m):
-        slots = pl.ds(side * 4 + part * 2, 2)
+        slots = pl.ds(side * 4, 4) if part is None else pl.ds(side * 4 + part * 2, 2)
         return part_out.at[slots, m], part_in.at[slots, m]
 
     def gfield_ends(side, part, t):
         own, other = (1, 3) if side == 0 else (2, 0)
         rows = pl.ds(pl.multiple_of(t * 16, 16), 16)
-        half_members = pl.ds(part * (members // 2), members // 2)
-        return grad_field.at[half_members, own, rows], grad_field.at[half_members, other, rows]
+        which = pl.ds(0, members) if part is None else pl.ds(part * (members // 2), members // 2)
+        return grad_field.at[which, own, rows], grad_field.at[which, other, rows]
 
     def hgrad_ends(side, part, m):
         own, other = (1, 3) if side == 0 else (2, 0)
@@ -127,16 +127,16 @@
     def direct(kind, side, part, m, where):
         ends, ss, rs, _, _ = kind
         src, dst = ends(side, part, m)
-        return remote(src, dst, ss.at[side * 2 + part, m], rs.at[side * 2 + part, m], lat=where)
+        return remote(src, dst, ss.at[side, m], rs.at[side, m], lat=where)
 
     def to_relay(kind, side, m, where):
         ends, ss, _, buffer, row = kind
-        return remote(ends(side, 1, m)[0], buffer.at[m], ss.at[side * 2 + 1, m], relay_r.at[row, m], lat=where)
+        return remote(ends(side, 1, m)[0], buffer.at[m], ss.at[side, m], relay_r.at[row, m], lat=where)
 
     def from_relay(kind, side, m):
         ends, _, rs, buffer, row = kind
         return remote(
-            buffer.at[m], ends(side, 1, m)[1], relay_s.at[row, m], rs.at[side * 2 + 1, m], lat=relay_end
+            buffer.at[m], ends(side, 1, m)[1], relay_s.at[row, m], rs.at[side, m], lat=relay_end
         )
 
     def send_halo(kind, m):
@@ -155,15 +155,13 @@
         for side, _, receives, where, _, _ in sides:
             @pl.when(receives)
             def _():
-                direct(kind, side, 0, m, where).wait_recv()
-                direct(kind, side, 1, m, where).wait_recv()
+                direct(kind, side, None, m, where).wait_recv()
 
     def drain_halo(kind, m):
         for side, sends, _, where, _, _ in sides:
             @pl.when(sends)
             def _():
-                direct(kind, side, 0, m, where).wait_send()
-                direct(kind, side, 1, m, where).wait_send()
+                direct(kind, side, None, m, where).wait_send()
 
         for side, relay in ((0, relay_up), (1, relay_down)):
             @pl.when(r == relay)
@@ -178,8 +176,9 @@
                 from_relay(kind, side, m).start()
 
     for m in range(members):
-        for row in range(2):
-            load(m, row).wait()
+        pltpu.make_async_copy(
+            feat.at[m], feat_rows.at[pl.ds(1, 2), m, pl.ds(0, lon)], load_sem.at[m]
+        ).wait()
         send_halo(feat_halo, m)
 
     feat_rows[:, :, lon:, :] = jnp.zeros((4, members, lon_pad - lon, LANE), BF16)
@@ -285,7 +284,7 @@
         p = mem_peer(k)
         return remote(
             field_out.at[p, m, tile(t)], values_in.at[d, m, tile(t)],
-            a2_s.at[m * chunks + t, k], a2_r.at[m * chunks + t, k], mem=p,
+            a2_s.at[t], a2_r.at[t], mem=p,
         )
 
     def finish_field(m):
@@ -302,11 +301,16 @@
                 field_copy(m, t, k).start()
         values_in[d, m] = field_out[d, m]
 
-    for m in range(members):
-        pass_on(feat_halo, m)
+    pass_on(feat_halo, 0)
+    pass_on(feat_halo, 1)
 
     def forward_step(m, carry):
         forward(m)
+
+        @pl.when(m == 0)
+        def _():
+            for n in range(2, members):
+                pass_on(feat_halo, n)
 
         @pl.when(m > 0)
         def _():
@@ -336,7 +340,7 @@
         return remote(
             grad_out.at[p, :, rows],
             grad_field.at[:, own_row, rows, pl.ds(pl.multiple_of(own_lane, LANE), third)],
-            b2_s.at[t, k], b2_r.at[t, k], mem=p,
+            b2_s.at[t], b2_r.at[t], mem=p,
         )
 
     block = 8
@@ -346,12 +350,11 @@
     def pair_chunk(t, carry):
         rows16 = tile(t)
 
-        def arrived(m, inner):
-            for k in range(1, MEM):
-                field_copy(m, t, k).wait()
-            return inner
-
-        lax.fori_loop(0, members, arrived, 0)
+        others = pl.ds(0, MEM - 1)
+        remote(
+            field_out.at[others, :, rows16], values_in.at[others, :, rows16],
+            a2_s.at[t], a2_r.at[t], mem=mem_peer(1),
+        ).wait()
         scale = jnp.concatenate([prm[0, rows16]] * lane_groups, axis=1)
         for j in range(count):
             rows, cols = place(j)
@@ -416,9 +419,17 @@
     lax.fori_loop(0, chunks, pair_chunk, 0)
 
     def wait_back(t, carry):
-        for k in range(1, MEM):
-            back_copy(t, k).wait()
+        others = pl.ds(0, MEM - 1)
+        remote(
+            grad_out.at[others, :, tile(t)], values_in.at[others, :, tile(t)],
+            b2_s.at[t], b2_r.at[t], mem=mem_peer(1),
+        ).wait()
         send_halo(gfield_halo, t)
+
+        @pl.when(t > 0)
+        def _():
+            pass_on(gfield_halo, t - 1)
+
         return carry
 
     lax.fori_loop(0, chunks, wait_back, 0)
@@ -434,36 +445,40 @@
         piece_rows = half_rows // MEM
         my_half = half * half_rows
         my_piece = my_half + d * piece_rows
-        s1, s2, s3, s4, s5 = [(sems.at[2 * n], sems.at[2 * n + 1]) for n in range(5)]
 
         def scatter_pair():
             return remote(
-                src.at[at_rows((1 - half) * half_rows, half_rows)], r1, s1[0].at[0], s1[1].at[0], lat=partner
+                src.at[at_rows((1 - half) * half_rows, half_rows)], r1, sems.at[0], sems.at[1], lat=partner
             )
 
         def scatter(k):
             return remote(
                 src.at[at_rows(my_half + mem_peer(k) * piece_rows, piece_rows)],
-                r2.at[k], s2[0].at[k], s2[1].at[k], mem=mem_peer(k),
+                r2.at[k], sems.at[2], sems.at[3], mem=mem_peer(k),
             )
 
         def share(k):
-            return remote(src.at[at_rows(my_piece, piece_rows)], r3.at[seat], s3[0].at[k], s3[1].at[k], lat=lat_peer(k))
+            return remote(src.at[at_rows(my_piece, piece_rows)], r3.at[seat], sems.at[4], sems.at[5], lat=lat_peer(k))
 
         def gather(k):
             piece = dst.at[at_rows(my_piece, piece_rows)]
-            return remote(piece, piece, s4[0].at[k], s4[1].at[k], mem=mem_peer(k))
+            return remote(piece, piece, sems.at[6], sems.at[7], mem=mem_peer(k))
 
         def gather_pair():
             piece = dst.at[at_rows(my_half, half_rows)]
-            return remote(piece, piece, s5[0].at[0], s5[1].at[0], lat=partner)
+            return remote(piece, piece, sems.at[8], sems.at[9], lat=partner)
 
         def each(copy_of, act):
             for k in range(1, MEM):
                 act(copy_of(k))
 
         start = lambda c: c.start()
-        wait = lambda c: c.wait()
+
+        def wait_all(n, where):
+            size = (MEM - 1) * piece_rows
+            remote(
+                src.at[pl.ds(0, size)], dst.at[pl.ds(0, size)], sems.at[2 * n], sems.at[2 * n + 1], **where
+            ).wait()
 
         def step_0():
             scatter_pair().start()
@@ -475,7 +490,7 @@
             each(scatter, start)
 
         def step_2():
-            each(scatter, wait)
+            wait_all(1, {"mem": mem_peer(1)})
             mine = at_rows(my_piece, piece_rows)
             total = src[mine]
             for k in range(1, MEM):
@@ -485,7 +500,7 @@
             r3[seat] = total
 
         def step_3():
-            each(share, wait)
+            wait_all(2, {"lat": lat_peer(1)})
             total = r3[0]
             for k in range(1, MEM):
                 total = total + r3[k]
@@ -493,7 +508,7 @@
             each(gather, start)
 
         def step_4():
-            each(gather, wait)
+            wait_all(3, {"mem": mem_peer(1)})
             gather_pair().start()
 
         def step_5():
@@ -510,10 +525,10 @@
         return carry
 
     def halo_tiles(t, carry):
-        pass_on(gfield_halo, t)
         recv_halo(gfield_halo, t)
         return carry
 
+    pass_on(gfield_halo, chunks - 1)
     lax.fori_loop(0, chunks, halo_tiles, 0)
     lax.fori_loop(0, members, head_gradient, 0)
     for a in range(3):
@@ -571,7 +586,6 @@
         return pltpu.make_async_copy(gf_buf.at[lax.rem(m, 2)], gf_out.at[m], out_sem.at[lax.rem(m, 2)])
 
     inner_steps[0]()
-    pass_on(hgrad_halo, members - 1)
 
     def last(m, carry):
         recv_halo(hgrad_halo, m)
@@ -597,6 +611,8 @@
                 if n > 0:
                     head_steps[n + 1]()
                 inner_steps[n + 1]()
+                if n == 0:
+                    pass_on(hgrad_halo, members - 1)
 
         return carry
 
@@ -670,14 +686,14 @@
         pltpu.VMEM((VP, third), F32),
         *sum_scratch(HEAD_ROWS),
         *sum_scratch(9 * LANE),
-        dma((members, 2)),
-        dma((4, members)), dma((4, members)),
-        dma((4, members)), dma((4, members)),
-        dma((members * VP // 16, MEM)), dma((members * VP // 16, MEM)),
-        dma((VP // 16, MEM)), dma((VP // 16, MEM)),
-        dma((4, VP // 16)), dma((4, VP // 16)),
-        dma((4, members)), dma((4, members)),
-        dma((10, MEM)), dma((10, MEM)),
+        dma((members,)),
+        dma((2, members)), dma((2, members)),
+        dma((2, members)), dma((2, members)),
+        dma((VP // 16,)), dma((VP // 16,)),
+        dma((VP // 16,)), dma((VP // 16,)),
+        dma((2, VP // 16)), dma((2, VP // 16)),
+        dma((2, members)), dma((2, members)),
+        dma((10,)), dma((10,)),
         dma((2,)),
         dma((4, VP // 16)), dma((4, VP // 16)),
     ]

time: 143 us -> 135 us (0.944)
  Pallas kernels: 137 us -> 129 us
    pallas_call x1, Pallas kernels: 137 us -> 129 us  [shards(): pl.pallas_call(whole_block, out_shape=(jax.ShapeDtypeStruct(features.shap...]
where the time goes in v3:
time: 135 us
  Pallas kernels  129 us (96%)
  local copies, waits for them, and re-layouts  5.25 us (4%)
    pallas_call x1, Pallas kernels, shards(): pl.pallas_call(whole_block, out_shape=(jax.ShapeDtypeStruct(features.shap...  129 us
    unnamed x7, local copies, waits for them, and re-layouts  5.25 us

profile of v3, /device:TPU:1, one launch (start us, length us, event | category | flops | bytes accessed | tf_op | source)
XLA Modules:
  0.0 134.9 jit_solution(15102571320455387115)
XLA Ops:
  0.6 129.0 %shard_map.85 = (bf16[4,2,1440,128]{3,2,1,0:T(8,128)(2,1)}, f32[9,128,128]{2,1,0:T(8,128)}, f32[9,69,128]{2,1,0:T(8,128)}) custom-call(bf16[4,2,1440,128]{3,2,1,0:T(8,128)(2,1)} %feat.1, bf16[9,128,128]{2,1,0:T(8,128)(2,1)} %bitcast.12, bf16[9,69,128]{2,1,0:T(8,128)(2,1)} %bitcast.13, f32[1,69]{1,0:T(1,128)} %bitcast.14, f32[1,69]{1,0:T(1,128)} %bitcast.15, ...), custom_call_target="tpu_custom_call" | custom-call | tf_op jit(solution)/shard_map/pallas_call | solution.py:700
  129.7 0.0 copy-start
  129.7 0.0 copy-start.1
  129.7 3.7 %copy.12 = bf16[4,2,1440,128]{3,2,1,0:T(8,128)(2,1)} copy(bf16[4,2,1440,128]{3,2,1,0:T(8,128)(2,1)} %get-tuple-element.12) | data formatting | bytes 5898240
  133.4 0.0 copy-done
  133.4 0.8 copy.13
  134.2 0.0 copy-done.1
  134.2 0.7 copy.14
Async XLA Ops:
  129.7 3.7 %copy-start = (f32[9,128,128]{2,1,0:T(8,128)S(1)}, f32[9,128,128]{2,1,0:T(8,128)}, u32[]{:S(2)}) copy-start(f32[9,128,128]{2,1,0:T(8,128)} %get-tuple-element.7) | copy-start | bytes 1769476
  129.7 4.5 %copy-start.1 = (f32[9,69,128]{2,1,0:T(8,128)S(1)}, f32[9,69,128]{2,1,0:T(8,128)}, u32[]{:S(2)}) copy-start(f32[9,69,128]{2,1,0:T(8,128)} %get-tuple-element.8) | copy-start | bytes 953860

commit v4 on v3

--- a/solution.py
+++ b/solution.py
@@ -35,7 +35,8 @@
     w_inner, w_head, w_head_back, w_inner_back,
     feat_relay, part_relay, gfield_relay, hgrad_relay,
     inner_acc, head_acc, gf_buf, prm, target_buf,
-    hs_in, hs_out, hs_r1, hs_r2, hs_r3, is_in, is_out, is_r1, is_r2, is_r3,
+    hs_in, hs_out, hs_r1, hs_r2, hs_r3, hs_sb, hs_db,
+    is_in, is_out, is_r1, is_r2, is_r3, is_sb, is_db,
     load_sem, fh_s, fh_r, ph_s, ph_r, a2_s, a2_r, b2_s, b2_r, gh_s, gh_r, hh_s, hh_r,
     hsum_sems, isum_sems, out_sem, relay_s, relay_r,
 ):
@@ -440,7 +441,7 @@
     def at_rows(start, size):
         return pl.ds(pl.multiple_of(start, 8), size)
 
-    def device_sum(src, dst, r1, r2, r3, sems):
+    def device_sum(src, dst, r1, r2, r3, sb, db, sems):
         half_rows = src.shape[0] // 2
         piece_rows = half_rows // MEM
         my_half = half * half_rows
@@ -453,19 +454,18 @@
 
         def scatter(k):
             return remote(
-                src.at[at_rows(my_half + mem_peer(k) * piece_rows, piece_rows)],
-                r2.at[k], sems.at[2], sems.at[3], mem=mem_peer(k),
+                sb.at[mem_peer(k)], r2.at[k], sems.at[2], sems.at[3], mem=mem_peer(k),
             )
 
         def share(k):
-            return remote(src.at[at_rows(my_piece, piece_rows)], r3.at[seat], sems.at[4], sems.at[5], lat=lat_peer(k))
+            return remote(r3.at[seat], r3.at[seat], sems.at[4], sems.at[5], lat=lat_peer(k))
 
         def gather(k):
-            piece = dst.at[at_rows(my_piece, piece_rows)]
+            piece = db.at[half, d]
             return remote(piece, piece, sems.at[6], sems.at[7], mem=mem_peer(k))
 
         def gather_pair():
-            piece = dst.at[at_rows(my_half, half_rows)]
+            piece = db.at[half]
             return remote(piece, piece, sems.at[8], sems.at[9], lat=partner)
 
         def each(copy_of, act):
@@ -474,11 +474,9 @@
 
         start = lambda c: c.start()
 
-        def wait_all(n, where):
-            size = (MEM - 1) * piece_rows
-            remote(
-                src.at[pl.ds(0, size)], dst.at[pl.ds(0, size)], sems.at[2 * n], sems.at[2 * n + 1], **where
-            ).wait()
+        def wait_all(n, buffer, where):
+            slabs = buffer.at[pl.ds(0, MEM - 1)]
+            remote(slabs, slabs, sems.at[2 * n], sems.at[2 * n + 1], **where).wait()
 
         def step_0():
             scatter_pair().start()
@@ -487,37 +485,42 @@
             scatter_pair().wait()
             mine = at_rows(my_half, half_rows)
             src[mine] = src[mine] + r1[...]
+            for p in range(MEM):
+                sb[p] = src[at_rows(my_half + p * piece_rows, piece_rows)].astype(BF16)
             each(scatter, start)
 
         def step_2():
-            wait_all(1, {"mem": mem_peer(1)})
+            wait_all(1, r2, {"mem": mem_peer(1)})
             mine = at_rows(my_piece, piece_rows)
             total = src[mine]
             for k in range(1, MEM):
-                total = total + r2[k]
-            src[mine] = total
+                total = total + r2[k].astype(F32)
+            r3[seat] = total.astype(BF16)
             each(share, start)
-            r3[seat] = total
 
         def step_3():
-            wait_all(2, {"lat": lat_peer(1)})
-            total = r3[0]
+            wait_all(2, r3, {"lat": lat_peer(1)})
+            total = r3[0].astype(F32)
             for k in range(1, MEM):
-                total = total + r3[k]
-            dst[at_rows(my_piece, piece_rows)] = total * (1.0 / (2 * LAT * lon))
+                total = total + r3[k].astype(F32)
+            db[half, d] = (total * (1.0 / (2 * LAT * lon))).astype(BF16)
             each(gather, start)
 
         def step_4():
-            wait_all(3, {"mem": mem_peer(1)})
+            wait_all(3, db.at[0], {"mem": mem_peer(1)})
             gather_pair().start()
 
         def step_5():
             gather_pair().wait()
+            for h in range(2):
+                for p in range(MEM):
+                    start_row = h * half_rows + p * piece_rows
+                    dst[start_row:start_row + piece_rows] = db[h, p].astype(F32)
 
         return step_0, step_1, step_2, step_3, step_4, step_5
 
-    head_steps = device_sum(hs_in, hs_out, hs_r1, hs_r2, hs_r3, hsum_sems)
-    inner_steps = device_sum(is_in, is_out, is_r1, is_r2, is_r3, isum_sems)
+    head_steps = device_sum(hs_in, hs_out, hs_r1, hs_r2, hs_r3, hs_sb, hs_db, hsum_sems)
+    inner_steps = device_sum(is_in, is_out, is_r1, is_r2, is_r3, is_sb, is_db, isum_sems)
 
     def head_gradient(m, carry):
         fields = grad_field[m].reshape(4 * VP, lon_pad)
@@ -563,13 +566,14 @@
         send_halo(hgrad_halo, m)
         rows = jnp.concatenate([feat_rows[e, m] for e in range(4)], axis=1)
         inner_acc[...] += jnp.dot(hgrad_t[...], rows, preferred_element_type=F32)
-        @pl.when(m >= 1)
+        @pl.when(m >= 2)
         def _():
-            pass_on(hgrad_halo, m - 1)
-
-        @pl.when(m == 1)
-        def _():
-            head_steps[1]()
+            pass_on(hgrad_halo, m - 2)
+
+        for n in (1, 2):
+            @pl.when(m == 2 * n - 1)
+            def _():
+                head_steps[n]()
 
         return carry
 
@@ -608,10 +612,11 @@
         for n in range(members):
             @pl.when(m == n)
             def _():
+                inner_steps[n + 1]()
                 if n > 0:
-                    head_steps[n + 1]()
-                inner_steps[n + 1]()
+                    head_steps[n + 2]()
                 if n == 0:
+                    pass_on(hgrad_halo, members - 2)
                     pass_on(hgrad_halo, members - 1)
 
         return carry
@@ -626,7 +631,6 @@
         drain_halo(gfield_halo, t)
     for m in range(max(members - 2, 0), members):
         gf_copy(m).wait()
-    head_steps[5]()
     for ab in range(9):
         gh_out[ab] = hs_out[ab * VP:ab * VP + gh_out.shape[1]]
     inner_steps[5]()
@@ -640,8 +644,10 @@
         pltpu.VMEM((rows, LANE), F32),
         pltpu.VMEM((rows, LANE), F32),
         pltpu.VMEM((rows // 2, LANE), F32),
-        pltpu.VMEM((MEM, piece, LANE), F32),
-        pltpu.VMEM((MEM, piece, LANE), F32),
+        pltpu.VMEM((MEM, piece, LANE), BF16),
+        pltpu.VMEM((MEM, piece, LANE), BF16),
+        pltpu.VMEM((MEM, piece, LANE), BF16),
+        pltpu.VMEM((2, MEM, piece, LANE), BF16),
     ]
 
 

time: 135 us -> 129 us (0.956)
  Pallas kernels: 129 us -> 123 us
    pallas_call x1, Pallas kernels: 129 us -> 123 us  [shards(): pl.pallas_call(whole_block, out_shape=(jax.ShapeDtypeStruct(features.shap...]
where the time goes in v4:
time: 129 us
  Pallas kernels  123 us (95%)
  local copies, waits for them, and re-layouts  5.25 us (4%)
    pallas_call x1, Pallas kernels, shards(): pl.pallas_call(whole_block, out_shape=(jax.ShapeDtypeStruct(features.shap...  123 us
    unnamed x7, local copies, waits for them, and re-layouts  5.25 us

profile of v4, /device:TPU:1, one launch (start us, length us, event | category | flops | bytes accessed | tf_op | source)
XLA Modules:
  0.0 128.7 jit_solution(11967921171158671272)
XLA Ops:
  0.6 122.8 %shard_map.85 = (bf16[4,2,1440,128]{3,2,1,0:T(8,128)(2,1)}, f32[9,128,128]{2,1,0:T(8,128)}, f32[9,69,128]{2,1,0:T(8,128)}) custom-call(bf16[4,2,1440,128]{3,2,1,0:T(8,128)(2,1)} %feat.1, bf16[9,128,128]{2,1,0:T(8,128)(2,1)} %bitcast.12, bf16[9,69,128]{2,1,0:T(8,128)(2,1)} %bitcast.13, f32[1,69]{1,0:T(1,128)} %bitcast.14, f32[1,69]{1,0:T(1,128)} %bitcast.15, ...), custom_call_target="tpu_custom_call" | custom-call | tf_op jit(solution)/shard_map/pallas_call | solution.py:706
  123.4 0.0 copy-start
  123.4 0.0 copy-start.1
  123.5 3.7 %copy.12 = bf16[4,2,1440,128]{3,2,1,0:T(8,128)(2,1)} copy(bf16[4,2,1440,128]{3,2,1,0:T(8,128)(2,1)} %get-tuple-element.12) | data formatting | bytes 5898240
  127.2 0.0 copy-done
  127.2 0.8 copy.13
  128.0 0.0 copy-done.1
  128.0 0.7 copy.14
Async XLA Ops:
  123.4 3.7 %copy-start = (f32[9,128,128]{2,1,0:T(8,128)S(1)}, f32[9,128,128]{2,1,0:T(8,128)}, u32[]{:S(2)}) copy-start(f32[9,128,128]{2,1,0:T(8,128)} %get-tuple-element.7) | copy-start | bytes 1769476
  123.4 4.5 %copy-start.1 = (f32[9,69,128]{2,1,0:T(8,128)S(1)}, f32[9,69,128]{2,1,0:T(8,128)}, u32[]{:S(2)}) copy-start(f32[9,69,128]{2,1,0:T(8,128)} %get-tuple-element.8) | copy-start | bytes 953860

commit v5 on v4

--- a/solution.py
+++ b/solution.py
@@ -297,9 +297,21 @@
                     (1 - row) * 4 + q, m
                 ].astype(F32)
                 field_out[row * 4 + q, m] = total.astype(BF16)
-        for t in range(chunks):
-            for k in range(1, MEM):
-                field_copy(m, t, k).start()
+        early = members // 2
+
+        @pl.when(m < early)
+        def _():
+            for t in range(chunks):
+                for k in range(1, MEM):
+                    field_copy(m, t, k).start()
+
+        @pl.when(m == members - 1)
+        def _():
+            for t in range(chunks):
+                for late in range(early, members):
+                    for k in range(1, MEM):
+                        field_copy(late, t, k).start()
+
         values_in[d, m] = field_out[d, m]
 
     pass_on(feat_halo, 0)
@@ -420,17 +432,13 @@
     lax.fori_loop(0, chunks, pair_chunk, 0)
 
     def wait_back(t, carry):
+        pass_on(gfield_halo, t)
         others = pl.ds(0, MEM - 1)
         remote(
             grad_out.at[others, :, tile(t)], values_in.at[others, :, tile(t)],
             b2_s.at[t], b2_r.at[t], mem=mem_peer(1),
         ).wait()
         send_halo(gfield_halo, t)
-
-        @pl.when(t > 0)
-        def _():
-            pass_on(gfield_halo, t - 1)
-
         return carry
 
     lax.fori_loop(0, chunks, wait_back, 0)
@@ -531,7 +539,6 @@
         recv_halo(gfield_halo, t)
         return carry
 
-    pass_on(gfield_halo, chunks - 1)
     lax.fori_loop(0, chunks, halo_tiles, 0)
     lax.fori_loop(0, members, head_gradient, 0)
     for a in range(3):

time: 129 us -> 126 us (0.977)
  Pallas kernels: 123 us -> 120 us
    pallas_call x1, Pallas kernels: 123 us -> 120 us  [shards(): pl.pallas_call(whole_block, out_shape=(jax.ShapeDtypeStruct(features.shap...]
where the time goes in v5:
time: 126 us
  Pallas kernels  120 us (95%)
  local copies, waits for them, and re-layouts  5.25 us (4%)
    pallas_call x1, Pallas kernels, shards(): pl.pallas_call(whole_block, out_shape=(jax.ShapeDtypeStruct(features.shap...  120 us
    unnamed x7, local copies, waits for them, and re-layouts  5.25 us

profile of v5, /device:TPU:1, one launch (start us, length us, event | category | flops | bytes accessed | tf_op | source)
XLA Modules:
  0.0 125.6 jit_solution(7158849341916170286)
XLA Ops:
  0.6 119.7 %shard_map.85 = (bf16[4,2,1440,128]{3,2,1,0:T(8,128)(2,1)}, f32[9,128,128]{2,1,0:T(8,128)}, f32[9,69,128]{2,1,0:T(8,128)}) custom-call(bf16[4,2,1440,128]{3,2,1,0:T(8,128)(2,1)} %feat.1, bf16[9,128,128]{2,1,0:T(8,128)(2,1)} %bitcast.12, bf16[9,69,128]{2,1,0:T(8,128)(2,1)} %bitcast.13, f32[1,69]{1,0:T(1,128)} %bitcast.14, f32[1,69]{1,0:T(1,128)} %bitcast.15, ...), custom_call_target="tpu_custom_call" | custom-call | tf_op jit(solution)/shard_map/pallas_call | solution.py:713
  120.4 0.0 copy-start
  120.4 0.0 copy-start.1
  120.4 3.7 %copy.12 = bf16[4,2,1440,128]{3,2,1,0:T(8,128)(2,1)} copy(bf16[4,2,1440,128]{3,2,1,0:T(8,128)(2,1)} %get-tuple-element.12) | data formatting | bytes 5898240
  124.1 0.0 copy-done
  124.1 0.8 copy.13
  124.9 0.0 copy-done.1
  124.9 0.7 copy.14
Async XLA Ops:
  120.4 3.7 %copy-start = (f32[9,128,128]{2,1,0:T(8,128)S(1)}, f32[9,128,128]{2,1,0:T(8,128)}, u32[]{:S(2)}) copy-start(f32[9,128,128]{2,1,0:T(8,128)} %get-tuple-element.7) | copy-start | bytes 1769476
  120.4 4.5 %copy-start.1 = (f32[9,69,128]{2,1,0:T(8,128)S(1)}, f32[9,69,128]{2,1,0:T(8,128)}, u32[]{:S(2)}) copy-start(f32[9,69,128]{2,1,0:T(8,128)} %get-tuple-element.8) | copy-start | bytes 953860

commit v6 on v5

--- a/solution.py
+++ b/solution.py
@@ -402,15 +402,15 @@
                         sums[j] = -w if sums[j] is None else sums[j] - w
                 if i0 > 0:
                     sums = [s + wide[at(count + i0 + i)] for i, s in enumerate(sums)]
-                for j0 in range(i0 + block, count, 4):
-                    xj = [wide[at(j0 + j)] for j in range(4)]
-                    back = [None] * 4
-                    for j in range(4):
+                for j0 in range(i0 + block, count, block):
+                    xj = [wide[at(j0 + j)] for j in range(block)]
+                    back = [None] * block
+                    for j in range(block):
                         for i in range(block):
                             w = term(xj[j], xi[i])
                             sums[i] = sums[i] + w
                             back[j] = -w if back[j] is None else back[j] - w
-                    for j in range(4):
+                    for j in range(block):
                         old = back[j] if i0 == 0 else wide[at(count + j0 + j)] + back[j]
                         wide[at(count + j0 + j)] = old
                 for i in range(block):

time: 126 us -> 126 us (level)
  no operation moved by 1% of the time
where the time goes in v6:
time: 126 us
  Pallas kernels  120 us (95%)
  local copies, waits for them, and re-layouts  5.25 us (4%)
    pallas_call x1, Pallas kernels, shards(): pl.pallas_call(whole_block, out_shape=(jax.ShapeDtypeStruct(features.shap...  120 us
    unnamed x7, local copies, waits for them, and re-layouts  5.25 us

profile of v6, /device:TPU:1, one launch (start us, length us, event | category | flops | bytes accessed | tf_op | source)
XLA Modules:
  0.0 125.6 jit_solution(10532911483182492058)
XLA Ops:
  0.6 119.7 %shard_map.85 = (bf16[4,2,1440,128]{3,2,1,0:T(8,128)(2,1)}, f32[9,128,128]{2,1,0:T(8,128)}, f32[9,69,128]{2,1,0:T(8,128)}) custom-call(bf16[4,2,1440,128]{3,2,1,0:T(8,128)(2,1)} %feat.1, bf16[9,128,128]{2,1,0:T(8,128)(2,1)} %bitcast.12, bf16[9,69,128]{2,1,0:T(8,128)(2,1)} %bitcast.13, f32[1,69]{1,0:T(1,128)} %bitcast.14, f32[1,69]{1,0:T(1,128)} %bitcast.15, ...), custom_call_target="tpu_custom_call" | custom-call | tf_op jit(solution)/shard_map/pallas_call | solution.py:713
  120.4 0.0 copy-start
  120.4 0.0 copy-start.1
  120.4 3.7 %copy.12 = bf16[4,2,1440,128]{3,2,1,0:T(8,128)(2,1)} copy(bf16[4,2,1440,128]{3,2,1,0:T(8,128)(2,1)} %get-tuple-element.12) | data formatting | bytes 5898240
  124.1 0.0 copy-done
  124.1 0.8 copy.13
  124.9 0.0 copy-done.1
  124.9 0.7 copy.14
Async XLA Ops:
  120.4 3.7 %copy-start = (f32[9,128,128]{2,1,0:T(8,128)S(1)}, f32[9,128,128]{2,1,0:T(8,128)}, u32[]{:S(2)}) copy-start(f32[9,128,128]{2,1,0:T(8,128)} %get-tuple-element.7) | copy-start | bytes 1769476
  120.4 4.5 %copy-start.1 = (f32[9,69,128]{2,1,0:T(8,128)S(1)}, f32[9,69,128]{2,1,0:T(8,128)}, u32[]{:S(2)}) copy-start(f32[9,69,128]{2,1,0:T(8,128)} %get-tuple-element.8) | copy-start | bytes 953860
